TPU v7x, 512 devices: a whole 4x4x16 slice. The times are simulated.
512 devices in a mesh: seq: 128 (over y, z_lo, x), tp: 4 (over z_hi, core).
Axes of the slice: x: 4, y: 4, z: 16 (z_hi: 2, z_lo: 8; z = z_hi * 8 + z_lo), core: 2. Of those that a mesh axis runs over, the one named last changes fastest.
Arguments:
- queries: bfloat16 [6144, 2048], P('seq', 'tp'), may hold values from -16 to 16
- keys: bfloat16 [6144, 2048], P('seq', 'tp'), may hold values from -16 to 16
- values: bfloat16 [6144, 2048], P('seq', 'tp'), may hold values from -6 to 6
- patch_stream: bfloat16 [6144, 4096], P('seq', 'tp'), may hold values from -6 to 6
- out_weight: bfloat16 [2048, 4096], P('tp', 'seq'), may hold values from -1 to 1
- down_weight: bfloat16 [4096, 1280], P('tp'), may hold values from -0.09375 to 0.09375
- byte_states: bfloat16 [24576, 1280], P('seq', 'tp'), may hold values from -6 to 6
- patch_starts: int32 [128, 48], P('seq'), may hold values from 0 to 192, as said below
Outputs:
- new_patches: bfloat16 [6144, 4096], P('seq', 'tp')
- new_bytes: bfloat16 [24576, 1280], P('seq', 'tp')
Inputs may be any that keep to these rules, and one draw needn't show every extreme that they name: `patch_starts`: each row d lists rising offsets within device d's 192 bytes at which patches start: the first is 0 in row 0 and from 4 to 7 in the other rows, the others are 8 or more; at least 24 entries of a row are offsets, some row has all 48, and the remaining entries at the end of a row equal 192.
All inputs are finite; a program needn't handle non-finite values.
Results may differ from a plain program's by a relative error of at most 0.015.
Values may be sent and summed in bfloat16 or wider, within the bound.
No kernel may reach another device: no remote copies, remote signals or barrier semaphores. Data moves between devices by JAX's collectives and lax.ppermute only.
A program may use at most 128 MiB of HBM per device.

v0:
```python
import jax
import jax.numpy as jnp
from jax import lax
from jax.sharding import Mesh
from jax.sharding import PartitionSpec as P

DH = 128
B_DEV = 192
SEQ = ("seq_0", "seq_1", "seq_2")


NEG = -1e30


def side_by_side(arrays, axis, dim, along):
    columns = [a.reshape(*a.shape[:along], -1) for a in arrays]
    both = jnp.concatenate(columns, axis=along)
    whole, at, finished = (lax.all_gather(both, axis, axis=dim, tiled=True), 0, [])
    for a, column in zip(arrays, columns):
        section = whole[..., at : at + column.shape[along]]
        finished.append(section.reshape(*section.shape[:along], *a.shape[along:]))
        at += column.shape[along]
    return tuple(finished)


def in_order(blocks, dim):
    dims = list(blocks.shape[1:])
    dims[dim] *= blocks.shape[0]
    return jnp.moveaxis(blocks, 0, dim).reshape(dims)


def gather_in_order(value, axes, turns):
    blocks = value[None]
    for k in turns:
        blocks = lax.all_gather(blocks, axes[k], axis=0, tiled=True)
    held = [lax.axis_size(axes[k]) for k in reversed(turns)]
    blocks = blocks.reshape(*held, *value.shape)
    turned = sorted(range(len(turns)), key=lambda place: turns[len(turns) - 1 - place])
    return blocks.transpose(*turned, *range(len(turns), blocks.ndim)).reshape(-1, *value.shape)


def gathered_by_axis(value, axes, turns, dim):
    return in_order(gather_in_order(value, axes, turns), dim)


def split_up(value, dim, devices):
    dims = value.shape
    blocks = value.reshape(*dims[:dim], devices, dims[dim] // devices, *dims[dim + 1 :])
    return jnp.moveaxis(blocks, dim, 0)


def sum_at_owner(value, axis, dim):
    blocks = split_up(value, dim, lax.axis_size(axis))
    arrived = lax.all_to_all(blocks, axis, split_axis=0, concat_axis=0, tiled=True)
    return arrived.astype(jnp.float32).sum(axis=0)


def from_behind(value, axis, by):
    devices = lax.axis_size(axis)
    pairs = [(i, i + by) for i in range(devices) if 0 <= i + by < devices]
    return lax.ppermute(value, axis, pairs)


def on_device(
    queries, keys, values, patch_stream, out_weight, down_weight, byte_states, patch_starts
):
    rows = queries.shape[0]
    width = queries.shape[1]
    heads = width // DH
    scale = DH ** (-0.5)
    starts_row = patch_starts.reshape(-1)
    valid = starts_row < B_DEV
    key_mask = valid.astype(jnp.bfloat16)
    first_slot = lax.axis_index(SEQ) * rows
    query_ids = first_slot + jnp.arange(rows, dtype=jnp.int32)
    query_heads = queries.reshape(rows, heads, DH)

    def attend(carry, piece):
        peak, total, summed = carry
        key_piece, value_piece, mask_piece = piece
        count = key_piece.shape[0]
        key_heads = key_piece.reshape(count, heads, DH)
        value_heads = value_piece.reshape(count, heads, DH)
        scores = (
            jnp.einsum("qhd,khd->hqk", query_heads, key_heads, preferred_element_type=jnp.float32)
            * scale
        )
        key_ids = jnp.arange(count, dtype=jnp.int32)
        allowed = (mask_piece > 0)[None, :] & (key_ids[None, :] <= query_ids[:, None])
        scores = jnp.where(allowed[None], scores, NEG)
        new_peak = jnp.maximum(peak, jnp.max(scores, axis=-1))
        expo = jnp.exp(scores - new_peak[:, :, None])
        total = jnp.sum(expo, axis=-1)
        weights = expo.astype(jnp.bfloat16)
        summed = jnp.einsum(
            "hqk,khd->hqd", weights, value_heads, preferred_element_type=jnp.float32
        )
        return (new_peak, total, summed)

    last_slot = first_slot + rows - 1
    start_state = (
        jnp.full((heads, rows), NEG, jnp.float32),
        jnp.zeros((heads, rows), jnp.float32),
        jnp.zeros((heads, rows, DH), jnp.float32),
    )
    piece = side_by_side((keys, values, key_mask), SEQ, 0, 1)
    peak, total, summed = lax.cond(
        jnp.int32(0) > last_slot,
        lambda state: state,
        lambda state: attend(state, piece),
        start_state,
    )
    attn = summed / total[:, :, None]
    attn = jnp.transpose(attn, (1, 0, 2)).reshape(rows, width).astype(jnp.bfloat16)
    partial_value = jnp.dot(
        attn, gathered_by_axis(out_weight, SEQ, (1, 0, 2), 1), preferred_element_type=jnp.float32
    )
    mixed = sum_at_owner(partial_value.astype(jnp.bfloat16), "tp", 1)
    new_patches = (patch_stream.astype(jnp.float32) + mixed).astype(jnp.bfloat16)
    down_terms = jnp.dot(new_patches, down_weight, preferred_element_type=jnp.float32)
    patch_down = sum_at_owner(down_terms.astype(jnp.bfloat16), "tp", 1).astype(jnp.bfloat16)
    following = jnp.concatenate([valid[1:], jnp.zeros((1,), jnp.bool_)])
    last_pick = (valid & jnp.logical_not(following)).astype(jnp.bfloat16)[None, :]
    last_state = jnp.dot(last_pick, patch_down, preferred_element_type=jnp.float32).astype(
        jnp.bfloat16
    )
    earlier_state = from_behind(last_state, SEQ, 1)
    position = jnp.arange(B_DEV, dtype=jnp.int32)
    ends = jnp.concatenate([starts_row[1:], jnp.full((1,), B_DEV, jnp.int32)])
    member = (starts_row[None, :] <= position[:, None]) & (position[:, None] < ends[None, :])
    member = member.astype(jnp.bfloat16)
    before = (position < starts_row[0]).astype(jnp.float32)[:, None]
    added = jnp.dot(member, patch_down, preferred_element_type=jnp.float32)
    added = added + before * earlier_state.astype(jnp.float32)
    new_bytes = (byte_states.astype(jnp.float32) + added).astype(jnp.bfloat16)
    return (new_patches, new_bytes)


def solution(mesh):
    split = Mesh(mesh.devices.reshape(4, 8, 4, mesh.shape["tp"]), ("seq_0", "seq_1", "seq_2", "tp"))
    return jax.shard_map(
        on_device,
        mesh=split,
        in_specs=(
            P(SEQ, "tp"),
            P(SEQ, "tp"),
            P(SEQ, "tp"),
            P(SEQ, "tp"),
            P("tp", SEQ),
            P("tp", None),
            P(SEQ, "tp"),
            P(SEQ, None),
        ),
        out_specs=(P(SEQ, "tp"), P(SEQ, "tp")),
        check_vma=False,
    )
```

profile of v0, /device:TPU:2, one launch (start us, length us, event | category | flops | bytes accessed | tf_op | source)
XLA Modules:
  0.0 1229.7 jit_solution(483600808962983324)
XLA Ops:
  7.2 0.0 copy-start
  7.2 0.0 all-gather.7.cloned.1.call-start
  7.2 49.8 %all-gather = bf16[4096,32]{0,1:T(8,128)(2,1)S(1)} all-gather(bf16[512,32]{0,1:T(8,128)(2,1)} %param.14), channel_id=2, replica_groups=mesh['seq_0'=4,'seq_1'=8,'seq_2'=4,'tp'=4] {'seq_1'}, dimensions={0}, use_global_device_ids=true | all-gather | bytes 294912 | tf_op jit(solution)/shard_map/all_gather | solution.py:35
  57.0 0.8 copy.50
  57.8 0.0 all-gather.7.cloned.1.call-update
  57.8 0.0 all-gather.9.cloned.1.call-start
  57.9 33.7 %all-gather.7.cloned.1.call-done = bf16[32,512,32]{1,0,2:T(8,128)(2,1)} async-done(((bf16[8,512,32]{1,0,2:T(8,128)(2,1)}), bf16[32,512,32]{1,0,2:T(8,128)(2,1)}) %all-gather.7.cloned.1.call-update) | async-done | bytes 1048592 | tf_op jit(solution)/shard_map/all_gather | solution.py:35
  91.6 0.0 copy-start.3
  91.6 0.0 all-gather.9.cloned.1.call-update
  91.6 0.0 all-gather.5.cloned.1.call-start
  91.7 0.7 fusion.23
  92.3 0.1 copy.37
  92.4 1.5 pad_maximum_fusion
  93.9 0.0 all-gather.5.cloned.1.call-update
  94.0 55.4 %all-gather.9.cloned.1.call-done = bf16[128,512,32]{1,0,2:T(8,128)(2,1)} async-done(((bf16[32,512,32]{1,0,2:T(8,128)(2,1)}), bf16[128,512,32]{1,0,2:T(8,128)(2,1)}) %all-gather.9.cloned.1.call-update) | async-done | bytes 4194320 | tf_op jit(solution)/shard_map/all_gather | solution.py:35
  149.4 6.6 copy.41
  156.0 979.2 %all-gather.5.cloned.1.call-done = bf16[6144,1025]{1,0:T(8,128)(2,1)} async-done(((bf16[48,1025]{1,0:T(8,128)(2,1)}), bf16[6144,1025]{1,0:T(8,128)(2,1)}) %all-gather.5.cloned.1.call-update) | async-done | bytes 12595216 | tf_op jit(solution)/shard_map/all_gather | solution.py:18
  1135.2 0.0 copy-done.3
  1135.2 30.2 %conditional.1 = (f32[4,48]{1,0:T(4,128)S(1)}, f32[4,48,128]{2,1,0:T(8,128)S(1)}) conditional(s32[]{:T(128)} %convert_element_type.68, (bf16[6144,1025]{1,0:T(8,128)(2,1)}, s32[]{:T(128)}, s32[48]{0:T(128)S(1)}, bf16[48,512]{1,0:T(8,128)(2,1)S(1)}) %tuple.30, () %tuple.17), branch_computations={%region_0.3_spmd, %region_3.4_spmd} | conditional | flops 612833152 | bytes 77861968 | solution.py:107
  1135.2 18.4 %copy.38 = bf16[6144,1025]{0,1:T(8,128)(2,1)} copy(bf16[6144,1025]{1,0:T(8,128)(2,1)} %get-tuple-element.29) | data formatting | bytes 25190400 | tf_op jit(solution)/shard_map
  1153.6 5.5 fusion.27
  1159.1 1.0 compare_reduce_fusion
  1160.1 0.3 fusion.6
  1160.4 1.9 fusion.28
  1162.2 2.3 fusion.3
  1164.6 0.8 fusion.2
  1165.4 0.0 copy-start.4
  1165.4 0.0 copy-start.2
  1165.4 0.0 copy-start.5
  1165.4 3.6 convolution_convert_fusion
  1169.0 0.8 copy.63
  1169.7 6.0 all-to-all-start
  1175.7 0.0 copy-done.4
  1175.7 16.1 %all-to-all-done = bf16[4,48,1024]{2,1,0:T(8,128)(2,1)S(1)} async-done(((bf16[4,48,1024]{2,1,0:T(8,128)(2,1)}), bf16[4,48,1024]{2,1,0:T(8,128)(2,1)S(1)}, u32[]{:S(2)}, u32[]{:S(2)}) %all-to-all-start) | async-done | bytes 393248 | tf_op jit(solution)/shard_map/all_to_all | solution.py:54
  1191.9 0.1 convert_reduce_fusion
  1191.9 0.0 copy-done.2
  1192.0 0.0 copy-done
  1192.0 0.0 copy-start.1
  1192.0 0.6 convolution_convert_fusion.1
  1192.6 0.2 reshape.136
  1192.7 0.7 copy.64
  1193.4 3.3 all-to-all-start.1
  1196.8 0.1 slice_bitcast_fusion.1
  1196.9 0.1 slice_bitcast_fusion
  1197.0 13.3 %all-to-all-done.1 = bf16[4,48,320]{2,1,0:T(8,128)(2,1)S(1)} async-done(((bf16[4,48,320]{2,1,0:T(8,128)(2,1)}), bf16[4,48,320]{2,1,0:T(8,128)(2,1)S(1)}, u32[]{:S(2)}, u32[]{:S(2)}) %all-to-all-start.1) | async-done | bytes 122912 | tf_op jit(solution)/shard_map/all_to_all | solution.py:54
  1210.3 0.2 convolution_reduce_fusion
  1210.5 1.9 collective-permute-start
  1212.4 0.1 pad_add_fusion
  1212.5 9.8 collective-permute-done
  1222.3 0.0 copy-done.5
  1222.3 0.8 add_convert_fusion
  1223.2 0.0 copy-done.1
  (9 shorter events, 0.1 us)
Async XLA Ops:
  7.2 1184.8 %copy-start = (bf16[1024,1280]{1,0:T(8,128)(2,1)S(1)}, bf16[1024,1280]{1,0:T(8,128)(2,1)}, u32[]{:S(2)}) copy-start(bf16[1024,1280]{1,0:T(8,128)(2,1)} %param.15) | copy-start | bytes 7864324
  7.2 84.4 %all-gather.7.cloned.1.call-start = ((), (), s32[]{:S(2)}) async-start(), calls=%async_computation.3 | async-start | bytes 1310720 | tf_op jit(solution)/shard_map/all_gather | solution.py:35
  57.8 91.5 %all-gather.9.cloned.1.call-start = ((), (), s32[]{:S(2)}) async-start(), calls=%async_computation.4 | async-start | bytes 5242880 | tf_op jit(solution)/shard_map/all_gather | solution.py:35
  91.6 1043.6 %copy-start.3 = (bf16[48,512]{1,0:T(8,128)(2,1)S(1)}, bf16[48,512]{1,0:T(8,128)(2,1)}, u32[]{:S(2)}) copy-start(bf16[48,512]{1,0:T(8,128)(2,1)} %param.10) | copy-start | bytes 147460
  91.6 1043.6 %all-gather.5.cloned.1.call-start = ((), (), s32[]{:S(2)}) async-start(), calls=%async_computation.2 | async-start | bytes 14266368 | tf_op jit(solution)/shard_map/all_gather | solution.py:18
  1165.4 10.4 copy-start.4
  1165.4 26.6 %copy-start.2 = (bf16[48,1024]{1,0:T(8,128)(2,1)S(1)}, bf16[48,1024]{1,0:T(8,128)(2,1)}, u32[]{:S(2)}) copy-start(bf16[48,1024]{1,0:T(8,128)(2,1)} %param.13) | copy-start | bytes 294916
  1165.4 57.0 %copy-start.5 = (bf16[192,320]{1,0:T(8,128)(2,1)S(1)}, bf16[192,320]{1,0:T(8,128)(2,1)}, u32[]{:S(2)}) copy-start(bf16[192,320]{1,0:T(8,128)(2,1)} %param.16) | copy-start | bytes 368644
  1169.7 22.1 %all-to-all-start = ((bf16[4,48,1024]{2,1,0:T(8,128)(2,1)}), bf16[4,48,1024]{2,1,0:T(8,128)(2,1)S(1)}, u32[]{:S(2)}, u32[]{:S(2)}) async-start(bf16[4,48,1024]{2,1,0:T(8,128)(2,1)} %bitcast.59), calls=%async_computation | async-start | bytes 786432 | tf_op jit(solution)/shard_map/all_to_all | solution.py:54
  1192.0 31.2 %copy-start.1 = (bf16[48,1024]{1,0:T(8,128)(2,1)}, bf16[48,1024]{1,0:T(8,128)(2,1)S(1)}, u32[]{:S(2)}) copy-start(bf16[48,1024]{1,0:T(8,128)(2,1)S(1)} %add_convert_fusion.1) | copy-start | bytes 294916
  1193.4 16.8 %all-to-all-start.1 = ((bf16[4,48,320]{2,1,0:T(8,128)(2,1)}), bf16[4,48,320]{2,1,0:T(8,128)(2,1)S(1)}, u32[]{:S(2)}, u32[]{:S(2)}) async-start(bf16[4,48,320]{2,1,0:T(8,128)(2,1)} %bitcast.60), calls=%async_computation.1 | async-start | bytes 294912 | tf_op jit(solution)/shard_map/all_to_all | solution.py:54
  1210.5 11.8 collective-permute-start
Sparse Core Ops, SparseCore 0:
  57.9 33.6 all-gather.6
  93.7 55.6 all-gather.8
  152.0 983.1 all-gather.4
where the time goes:
time: 1230 us
  waiting for transfers between devices  1110 us (90%)
  blocking collectives  49.8 us (4%)
  local copies, waits for them, and re-layouts  33.2 us (3%)
  between operations  13.9 us (1%)
    all_gather x1, waiting for transfers between devices, side_by_side(): lax.all_gather(both, axis, axis=dim, tiled=True)  979 us
    all_gather x2, waiting for transfers between devices, gather_in_order(): blocks = lax.all_gather(blocks, axes[k], axis=0, tiled=True)  89.1 us
    all_gather x1, blocking collectives, gather_in_order(): blocks = lax.all_gather(blocks, axes[k], axis=0, tiled=True)  49.8 us
    all_to_all x2, waiting for transfers between devices, sum_at_owner(): lax.all_to_all(blocks, axis, split_axis=0, concat_axis=0, tiled=True)  29.4 us
  transfers between devices with their start and end apart: 6, of which 6 were waited for; matrix products, arithmetic and copies ran while one was open for 1% of the time, Pallas kernels for 0%

commit v1 on v0

v1 whole, which is shorter than its diff:
```python
import jax
import jax.numpy as jnp
from jax import lax
from jax.experimental import pallas as pl
from jax.experimental.pallas import tpu as pltpu
from jax.sharding import Mesh
from jax.sharding import PartitionSpec as P

DH = 128
B_DEV = 192
SEQ = ("y", "z", "x")
TP = ("h", "c")
PLANE = ("y", "x")
ROWS = 48
PAD = 56
NEG = -1e30
FLOOR = -1e29
MARK = 64.0
LIMIT = 4096.0
FAR = 1 << 30


def pieces(value):
    first = value.astype(jnp.bfloat16)
    rest = value - first.astype(jnp.float32)
    second = rest.astype(jnp.bfloat16)
    third = (rest - second.astype(jnp.float32)).astype(jnp.bfloat16)
    return [first, second, third]


def attend_kernel(place_ref, key_ids_ref, q_ref, near_ref, far_ref, out_ref):
    blocks, rows, width = q_ref.shape
    heads = width // DH
    kv = jnp.concatenate([near_ref[...].reshape(-1, 2 * width), far_ref[...].reshape(-1, 2 * width)], axis=0)
    ones = jnp.ones((8, DH), jnp.bfloat16)
    nt = (((1,), (1,)), ((), ()))
    marks = lax.dot_general(ones, kv[:, :DH], nt, preferred_element_type=jnp.float32)[:1]
    key_ids = jnp.where(marks > LIMIT, FAR, key_ids_ref[...] + place_ref[0])
    group = 4
    row = lax.rem(lax.broadcasted_iota(jnp.int32, (group * rows, 1), 0), rows)
    step = lax.div(lax.broadcasted_iota(jnp.int32, (group * rows, 1), 0), rows)
    row = jnp.where(row < ROWS, row, -1) + step * ROWS
    lane = lax.broadcasted_iota(jnp.int32, (group * rows, DH), 1)

    def one_group(index, _):
        device = index * 32 + place_ref[1]
        allowed = key_ids <= row + device * ROWS
        stats = jnp.zeros((group * rows, DH), jnp.float32)
        at_blocks = pl.ds(index * group, group)
        for h in range(heads):
            q = q_ref[at_blocks, :, h * DH : (h + 1) * DH].reshape(group * rows, DH)
            k = kv[:, h * DH : (h + 1) * DH]
            v = kv[:, width + h * DH : width + (h + 1) * DH]
            s = lax.dot_general(q, k, nt, preferred_element_type=jnp.float32) * (DH**-0.5)
            s = jnp.where(allowed, s, NEG)
            peak = jnp.maximum(jnp.max(s, axis=1, keepdims=True), FLOOR)
            e = jnp.exp(s - peak)
            total = jnp.sum(e, axis=1, keepdims=True)
            o = jnp.dot(e.astype(jnp.bfloat16), v, preferred_element_type=jnp.float32)
            out_ref[at_blocks, :, h * DH : (h + 1) * DH] = o.astype(jnp.bfloat16).reshape(group, rows, DH)
            for at, part in enumerate(pieces(peak) + pieces(total)):
                stats = jnp.where(lane == h * 6 + at, part.astype(jnp.float32), stats)
        out_ref[at_blocks, :, width:] = stats.astype(jnp.bfloat16).reshape(group, rows, DH)
        return 0

    lax.fori_loop(0, blocks // group, one_group, 0)


def combine_kernel(in_ref, out_ref):
    blocks, rows, width = in_ref.shape
    heads = (width - DH) // DH
    for h in range(heads):
        peaks, totals = [], []
        for b in range(blocks):
            stat = in_ref[b, :, heads * DH :].astype(jnp.float32)
            at = h * 6
            peaks.append(stat[:, at : at + 1] + stat[:, at + 1 : at + 2] + stat[:, at + 2 : at + 3])
            totals.append(stat[:, at + 3 : at + 4] + stat[:, at + 4 : at + 5] + stat[:, at + 5 : at + 6])
        top = peaks[0]
        for b in range(1, blocks):
            top = jnp.maximum(top, peaks[b])
        total = jnp.zeros_like(top)
        summed = jnp.zeros((rows, DH), jnp.float32)
        for b in range(blocks):
            share = jnp.exp(peaks[b] - top)
            total = total + share * totals[b]
            summed = summed + share * in_ref[b, :, h * DH : (h + 1) * DH].astype(jnp.float32)
        total = jnp.where(total > 0, total, 1.0)
        out_ref[:, h * DH : (h + 1) * DH] = (summed / total).astype(jnp.bfloat16)


VM = pl.BlockSpec(memory_space=pltpu.VMEM)
SM = pl.BlockSpec(memory_space=pltpu.SMEM)


def attend(place, key_ids, q, near, far):
    blocks, rows, width = q.shape
    return pl.pallas_call(
        attend_kernel,
        out_shape=jax.ShapeDtypeStruct((blocks, rows, width + DH), jnp.bfloat16),
        in_specs=[SM, VM, VM, VM, VM],
        out_specs=VM,
        cost_estimate=pl.CostEstimate(flops=4_000_000_000, bytes_accessed=3_000_000, transcendentals=1_400_000),
    )(place, key_ids, q, near, far)


def combine(parts):
    _, rows, width = parts.shape
    return pl.pallas_call(
        combine_kernel,
        out_shape=jax.ShapeDtypeStruct((rows, width - DH), jnp.bfloat16),
        in_specs=[VM],
        out_specs=VM,
        cost_estimate=pl.CostEstimate(flops=2_000_000_000, bytes_accessed=1_200_000, transcendentals=4_000),
    )(parts)


def exchange(value, axes):
    return lax.all_to_all(value, axes, split_axis=0, concat_axis=0, tiled=True)


def held_at(distance):
    return (distance & 1) * 4 + (distance & 2) + lax.div(distance, 4)


def project_kernel(place_ref, attn_ref, own_ref, less_ref, more_ref, low_ref, high_ref, stream_ref, down_ref, new_ref, keep_ref, send_ref):
    y, x, c, z = place_ref[0], place_ref[1], place_ref[2], place_ref[3]
    nt = (((1,), (1,)), ((), ()))
    span = 256
    heads = [attn_ref[lax.rem(y + step, 4)] for step in range(4)]
    turns = [lax.rem(x + 4 - source, 4) for source in range(4)]
    for at in range(stream_ref.shape[1] // span):
        total = stream_ref[:, at * span : (at + 1) * span].astype(jnp.float32)
        spots = [(turn, held_at((at * 2 + i) ^ z)) for i in range(2) for turn in turns]
        mixed = jnp.zeros_like(total)
        for attn, refs in zip(heads, ((own_ref,), (more_ref,), (low_ref, high_ref), (less_ref,))):
            weight = jnp.concatenate([ref[turn, spot] for turn, spot in spots for ref in refs], axis=0)
            mixed = mixed + lax.dot_general(attn, weight, nt, preferred_element_type=jnp.float32)
        new_ref[:, at * span : (at + 1) * span] = (total + mixed).astype(jnp.bfloat16)
    down = jnp.dot(new_ref[...], down_ref[...], preferred_element_type=jnp.float32)
    for half in range(2):
        at = half * 640
        first, second = down[:, at : at + 320], down[:, at + 320 : at + 640]
        keep_ref[half] = jnp.where(c == 0, first, second)
        send_ref[half] = jnp.where(c == 0, second, first).astype(jnp.bfloat16)


def project(place, attn, weights, stream, down_weight):
    rows, width = stream.shape
    return pl.pallas_call(
        project_kernel,
        out_shape=(
            jax.ShapeDtypeStruct((rows, width), jnp.bfloat16),
            jax.ShapeDtypeStruct((2, rows, 320), jnp.float32),
            jax.ShapeDtypeStruct((2, rows, 320), jnp.bfloat16),
        ),
        in_specs=[SM] + [VM] * 8,
        out_specs=(VM, VM, VM),
        cost_estimate=pl.CostEstimate(flops=4_000_000_000, bytes_accessed=7_000_000, transcendentals=0),
    )(place, attn, *weights, stream, down_weight)


def turned(value, axis, by):
    return lax.ppermute(value, axis, [(i, (i + by) % 4) for i in range(4)])


def line_halves(block):
    held = block[None]
    for bit in (4, 2, 1):
        other = lax.ppermute(held, "z", [(i, i ^ bit) for i in range(8)])
        if bit == 1:
            return held, other
        held = jnp.concatenate([held, other], axis=0)


def plane_gathered(blocks):
    own = jnp.stack([blocks] + [turned(blocks, "x", k) for k in (1, 2, 3)])
    less, more = turned(own, "y", 1), turned(own, "y", -1)
    return own, less, more, turned(less[:, :, :16], "y", 1), turned(more[:, :, 16:], "y", -1)


def across(value, axis):
    return lax.ppermute(value, axis, [(0, 1), (1, 0)])


def on_device(queries, keys, values, patch_stream, out_weight, down_weight, byte_states, patch_starts):
    y, z, x, h, c = (lax.axis_index(a) for a in (*SEQ, *TP))
    starts = patch_starts.reshape(-1)
    valid = starts < B_DEV
    count = jnp.sum(valid.astype(jnp.int32))
    pairs = [(a * 4 + t, t * 4 + a) for a in range(4) for t in range(4)]
    block = lax.ppermute(out_weight.T, ("y", "h", "c"), pairs)
    marked = jnp.where(valid[:, None], keys, jnp.bfloat16(MARK))
    kv = jnp.concatenate([marked, values], axis=1)
    blocks = jnp.concatenate(line_halves(block), axis=0)

    last = lax.dynamic_slice(jnp.concatenate([queries, patch_stream], axis=1), (count - 1, 0), (1, 1536))
    pairs = [(i, i + 1) for i in range(127)]
    earlier = lax.ppermute(last, SEQ, pairs)
    weights = plane_gathered(blocks)
    near, far = line_halves(kv)
    q = jnp.concatenate([queries, earlier[:, :512], jnp.zeros((PAD - ROWS - 1, 512), jnp.bfloat16)], axis=0)
    stream = jnp.concatenate([patch_stream, earlier[:, 512:], jnp.zeros((PAD - ROWS - 1, 1024), jnp.bfloat16)], axis=0)
    q = exchange(jnp.broadcast_to(q[None], (16, *q.shape)), PLANE)

    place = jnp.stack([(y * 32 + x) * ROWS, z * 4]).astype(jnp.int32)
    slot = jnp.arange(8 * ROWS, dtype=jnp.int32)
    away = slot // ROWS
    away = (away & 1) * 4 + (away & 2) + (away >> 2)
    key_ids = ((away ^ z) * (4 * ROWS) + slot % ROWS)[None]
    attn = combine(exchange(attend(place, key_ids, q, near, far), PLANE))

    attn = lax.all_gather(attn, TP, axis=0)
    new_rows, keep, send = project(jnp.stack([y, x, c, z]), attn, weights, stream, down_weight)
    both = keep + across(send, "c").astype(jnp.float32)
    here = jnp.where(h == 0, both[0], both[1])
    there = jnp.where(h == 0, both[1], both[0]).astype(jnp.bfloat16)
    patch_down = (here + across(there, "h").astype(jnp.float32)).astype(jnp.bfloat16)

    position = jnp.arange(B_DEV, dtype=jnp.int32)[:, None]
    begins = jnp.concatenate([starts, jnp.zeros((1,), jnp.int32), jnp.full((PAD - ROWS - 1,), B_DEV, jnp.int32)])
    ends = jnp.concatenate([starts[1:], jnp.full((1,), B_DEV, jnp.int32), starts[:1], jnp.full((PAD - ROWS - 1,), B_DEV, jnp.int32)])
    member = ((begins[None, :] <= position) & (position < ends[None, :])).astype(jnp.bfloat16)
    added = jnp.dot(member, patch_down, preferred_element_type=jnp.float32)
    new_bytes = (byte_states.astype(jnp.float32) + added).astype(jnp.bfloat16)
    return (new_rows[:ROWS], new_bytes)


def solution(mesh):
    split = Mesh(mesh.devices.reshape(4, 8, 4, 2, 2), ("y", "z", "x", "h", "c"))
    return jax.shard_map(
        on_device,
        mesh=split,
        in_specs=(
            P(SEQ, TP),
            P(SEQ, TP),
            P(SEQ, TP),
            P(SEQ, TP),
            P(TP, SEQ),
            P(TP, None),
            P(SEQ, TP),
            P(SEQ, None),
        ),
        out_specs=(P(SEQ, TP), P(SEQ, TP)),
        check_vma=False,
    )
```

time: 1230 us -> 177 us (0.14)
  the two profiles are of different devices: /device:TPU:2 before, /device:TPU:128 now
where the time goes in v1:
time: 177 us; the launch traced here: 176 us
  starting transfers between devices  91.2 us (52%)
  waiting for transfers between devices  31.3 us (18%)
  Pallas kernels  17.9 us (10%)
  blocking collectives  15.3 us (9%)
  other arithmetic  9.18 us (5%)
  local copies, waits for them, and re-layouts  7.68 us (4%)
  between operations  2.29 us (1%)
    all_to_all x2, starting transfers between devices, exchange(): return lax.all_to_all(value, axes, split_axis=0, concat_axis=0, tiled=True)  28.8 us
    ppermute x6, starting transfers between devices, line_halves(): other = lax.ppermute(held, 'z', [(i, i ^ bit) for i in range(8)])  25.4 us
    ppermute x7, starting transfers between devices, turned(): return lax.ppermute(value, axis, [(i, (i + by) % 4) for i in range(4)])  24.9 us
    ppermute x7, waiting for transfers between devices, turned(): return lax.ppermute(value, axis, [(i, (i + by) % 4) for i in range(4)])  20.4 us
    all_gather x1, blocking collectives, on_device(): attn = lax.all_gather(attn, TP, axis=0)  15.3 us
    ppermute x2, waiting for transfers between devices, across(): return lax.ppermute(value, axis, [(0, 1), (1, 0)])  8.98 us
    pallas_call x1, Pallas kernels, attend(): pl.pallas_call(attend_kernel, out_shape=jax.ShapeDtypeStruct((blocks, row...  8.16 us
    ppermute x2, starting transfers between devices, across(): return lax.ppermute(value, axis, [(0, 1), (1, 0)])  7.28 us
  transfers between devices with their start and end apart: 19, of which 5 were waited for; matrix products, arithmetic and copies ran while one was open for 6% of the time, Pallas kernels for 7%

profile of v1, /device:TPU:128, one launch (start us, length us, event | category | flops | bytes accessed | tf_op | source)
XLA Modules:
  0.0 175.8 jit_solution(1230273131034074662)
XLA Ops:
  0.6 1.3 convert_reduce_fusion
  3.2 0.7 fusion.9
  4.0 3.4 %collective-permute-start = (bf16[1,1536]{1,0:T(2,128)(2,1)S(1)}, bf16[1,1536]{1,0:T(2,128)(2,1)S(1)}, u32[]{:S(2)}, u32[]{:S(2)}) collective-permute-start(bf16[1,1536]{1,0:T(2,128)(2,1)S(1)} %fusion.9), channel_id=1, source_target_pairs={{0,4},{4,8},{8,12},{12,16},{16,20},{20,24},{24,28},{28,32},{32,36}... | collective-permute-start | bytes 9224 | tf_op jit(solution)/shard_map/ppermute | solution.py:199
  7.4 1.4 collective-permute-start.4
  8.8 0.7 broadcast_compare_fusion
  9.5 0.9 broadcast_select_fusion
  10.3 0.0 collective-permute-done.4
  10.3 3.9 %collective-permute-start.5 = (bf16[1,32,512]{2,1,0:T(8,128)(2,1)S(1)}, bf16[1,32,512]{2,1,0:T(8,128)(2,1)S(1)}, u32[]{:S(2)}, u32[]{:S(2)}) collective-permute-start(bf16[1,32,512]{2,1,0:T(8,128)(2,1)S(1)} %bitcast.31), channel_id=1, source_target_pairs={{0,64},{16,80},{32,96},{48,112},{64,0},{80,16},{96,32},{112,48},{1... | collective-permute-start | bytes 98312 | tf_op jit(solution)/shard_map/ppermute | solution.py:170
  14.2 0.8 maximum_bitcast_fusion
  15.0 5.8 %collective-permute-start.1 = (bf16[1,48,1024]{2,1,0:T(8,128)(2,1)S(1)}, bf16[1,48,1024]{2,1,0:T(8,128)(2,1)S(1)}, u32[]{:S(2)}, u32[]{:S(2)}) collective-permute-start(bf16[1,48,1024]{2,1,0:T(8,128)(2,1)S(1)} %maximum_bitcast_fusion), channel_id=1, source_target_pairs={{0,64},{16,80},{32,96},{48,112},{64,0},{80,16},{96,32},{112,48},{1... | collective-permute-start | bytes 294920 | tf_op jit(solution)/shard_map/ppermute | solution.py:170
  20.9 0.1 pad.32.clone
  21.0 0.0 collective-permute-done
  21.0 0.0 collective-permute-done.5
  21.0 5.2 %collective-permute-start.6 = (bf16[2,32,512]{2,1,0:T(8,128)(2,1)S(1)}, bf16[2,32,512]{2,1,0:T(8,128)(2,1)S(1)}, u32[]{:S(2)}, u32[]{:S(2)}) collective-permute-start(bf16[2,32,512]{2,1,0:T(8,128)(2,1)S(1)} %pad_maximum_fusion.5), channel_id=1, source_target_pairs={{0,32},{16,48},{32,0},{48,16},{64,96},{80,112},{96,64},{112,80},{1... | collective-permute-start | bytes 196616 | tf_op jit(solution)/shard_map/ppermute | solution.py:170
  26.2 0.9 maximum_maximum_fusion.1
  27.1 1.0 broadcast_in_dim.36
  28.1 25.1 %all-to-all-start = ((bf16[16,56,512]{2,1,0:T(8,128)(2,1)}), bf16[16,56,512]{2,1,0:T(8,128)(2,1)S(1)}, u32[]{:S(2)}, u32[]{:S(2)}) async-start(bf16[16,56,512]{2,1,0:T(8,128)(2,1)} %broadcast_in_dim.36), calls=%async_computation | async-start | bytes 1835008 | tf_op jit(solution)/shard_map/all_to_all | solution.py:119
  53.2 0.0 collective-permute-done.6
  53.2 4.2 %collective-permute-start.7 = (bf16[4,32,512]{2,1,0:T(8,128)(2,1)S(1)}, bf16[4,32,512]{2,1,0:T(8,128)(2,1)S(1)}, u32[]{:S(2)}, u32[]{:S(2)}) collective-permute-start(bf16[4,32,512]{2,1,0:T(8,128)(2,1)S(1)} %pad_maximum_fusion.4), channel_id=1, source_target_pairs={{0,16},{16,0},{32,48},{48,32},{64,80},{80,64},{96,112},{112,96},{1... | collective-permute-start | bytes 393224 | tf_op jit(solution)/shard_map/ppermute | solution.py:170
  57.5 0.0 collective-permute-done.1
  57.5 1.9 %collective-permute-start.2 = (bf16[2,48,1024]{2,1,0:T(8,128)(2,1)S(1)}, bf16[2,48,1024]{2,1,0:T(8,128)(2,1)S(1)}, u32[]{:S(2)}, u32[]{:S(2)}) collective-permute-start(bf16[2,48,1024]{2,1,0:T(8,128)(2,1)S(1)} %pad_maximum_fusion.3), channel_id=1, source_target_pairs={{0,32},{16,48},{32,0},{48,16},{64,96},{80,112},{96,64},{112,80},{1... | collective-permute-start | bytes 589832 | tf_op jit(solution)/shard_map/ppermute | solution.py:170
  59.4 1.9 %collective-permute-done.7 = bf16[4,32,512]{2,1,0:T(8,128)(2,1)S(1)} collective-permute-done((bf16[4,32,512]{2,1,0:T(8,128)(2,1)S(1)}, bf16[4,32,512]{2,1,0:T(8,128)(2,1)S(1)}, u32[]{:S(2)}, u32[]{:S(2)}) %collective-permute-start.7) | collective-permute-done | bytes 131104 | tf_op jit(solution)/shard_map/ppermute | solution.py:170
  61.3 4.8 %collective-permute-start.10 = (bf16[8,32,512]{2,1,0:T(8,128)(2,1)S(1)}, bf16[8,32,512]{2,1,0:T(8,128)(2,1)S(1)}, u32[]{:S(2)}, u32[]{:S(2)}) collective-permute-start(bf16[8,32,512]{2,1,0:T(8,128)(2,1)S(1)} %get-tuple-element.9), channel_id=1, source_target_pairs={{0,12},{4,0},{8,4},{12,8},{1,13},{5,1},{9,5},{13,9},{2,14},{6,2},{... | collective-permute-start | bytes 786440 | tf_op jit(solution)/shard_map/ppermute | solution.py:164
  66.1 2.8 %collective-permute-start.9 = (bf16[8,32,512]{2,1,0:T(8,128)(2,1)S(1)}, bf16[8,32,512]{2,1,0:T(8,128)(2,1)S(1)}, u32[]{:S(2)}, u32[]{:S(2)}) collective-permute-start(bf16[8,32,512]{2,1,0:T(8,128)(2,1)S(1)} %get-tuple-element.9), channel_id=1, source_target_pairs={{0,8},{4,12},{8,0},{12,4},{1,9},{5,13},{9,1},{13,5},{2,10},{6,14},... | collective-permute-start | bytes 786440 | tf_op jit(solution)/shard_map/ppermute | solution.py:164
  68.9 2.8 %collective-permute-start.8 = (bf16[8,32,512]{2,1,0:T(8,128)(2,1)S(1)}, bf16[8,32,512]{2,1,0:T(8,128)(2,1)S(1)}, u32[]{:S(2)}, u32[]{:S(2)}) collective-permute-start(bf16[8,32,512]{2,1,0:T(8,128)(2,1)S(1)} %get-tuple-element.9), channel_id=1, source_target_pairs={{0,4},{4,8},{8,12},{12,0},{1,5},{5,9},{9,13},{13,1},{2,6},{6,10},{... | collective-permute-start | bytes 786440 | tf_op jit(solution)/shard_map/ppermute | solution.py:164
  71.7 0.0 collective-permute-done.2
  71.8 4.4 %collective-permute-start.3 = (bf16[4,48,1024]{2,1,0:T(8,128)(2,1)S(1)}, bf16[4,48,1024]{2,1,0:T(8,128)(2,1)}, u32[]{:S(2)}, u32[]{:S(2)}) collective-permute-start(bf16[4,48,1024]{2,1,0:T(8,128)(2,1)S(1)} %pad_maximum_fusion.1.near_ref), channel_id=1, source_target_pairs={{0,16},{16,0},{32,48},{48,32},{64,80},{80,64},{96,112},{112,96},{1... | collective-permute-start | bytes 1179656 | tf_op jit(solution)/shard_map/ppermute | solution.py:170
  76.2 0.7 pad_add_fusion.3.place_ref
  76.8 0.6 fusion.10.key_ids_ref
  77.4 0.0 collective-permute-done.10
  77.4 0.0 collective-permute-done.9
  77.4 2.4 %collective-permute-done.8 = bf16[8,32,512]{2,1,0:T(8,128)(2,1)S(1)} collective-permute-done((bf16[8,32,512]{2,1,0:T(8,128)(2,1)S(1)}, bf16[8,32,512]{2,1,0:T(8,128)(2,1)S(1)}, u32[]{:S(2)}, u32[]{:S(2)}) %collective-permute-start.8) | collective-permute-done | bytes 262176 | tf_op jit(solution)/shard_map/ppermute | solution.py:164
  79.8 0.1 pad_maximum_fusion.own_ref
  80.0 3.4 %collective-permute-start.11 = (bf16[4,8,32,512]{3,2,1,0:T(8,128)(2,1)S(1)}, bf16[4,8,32,512]{3,2,1,0:T(8,128)(2,1)}, u32[]{:S(2)}, u32[]{:S(2)}) collective-permute-start(bf16[4,8,32,512]{3,2,1,0:T(8,128)(2,1)S(1)} %pad_maximum_fusion.own_ref), channel_id=1, source_target_pairs={{0,128},{128,256},{256,384},{384,0},{1,129},{129,257},{257,385},{3... | collective-permute-start | bytes 3145736 | tf_op jit(solution)/shard_map/ppermute | solution.py:164
  83.4 3.7 %collective-permute-start.12 = (bf16[4,8,32,512]{3,2,1,0:T(8,128)(2,1)S(1)}, bf16[4,8,32,512]{3,2,1,0:T(8,128)(2,1)}, u32[]{:S(2)}, u32[]{:S(2)}) collective-permute-start(bf16[4,8,32,512]{3,2,1,0:T(8,128)(2,1)S(1)} %pad_maximum_fusion.own_ref), channel_id=1, source_target_pairs={{0,384},{128,0},{256,128},{384,256},{1,385},{129,1},{257,129},{385... | collective-permute-start | bytes 3145736 | tf_op jit(solution)/shard_map/ppermute | solution.py:164
  87.1 0.0 collective-permute-done.3.far_ref
  87.1 1.0 copy-done.2
  88.0 8.2 %shard_map.95 = bf16[16,56,640]{2,1,0:T(8,128)(2,1)} custom-call(s32[2]{0:T(128)} %pad_add_fusion.3.place_ref, s32[1,384]{1,0:T(1,128)} %fusion.10.key_ids_ref, bf16[16,56,512]{2,1,0:T(8,128)(2,1)} %copy-done.2, bf16[4,48,1024]{2,1,0:T(8,128)(2,1)} %copy-done.3, bf16[4,48,1024]{2,1,0:T(8,128)(2,1)} %collective-permute-done.3.far_ref), custom_call_target="tpu_custom_call" | custom-call | flops 4000000000 | bytes 3000000 | tf_op jit(solution)/shard_map/pallas_call | solution.py:98
  96.2 3.7 %all-to-all-start.1 = ((bf16[16,56,640]{2,1,0:T(8,128)(2,1)}), bf16[16,56,640]{2,1,0:T(8,128)(2,1)S(1)}, u32[]{:S(2)}, u32[]{:S(2)}) async-start(bf16[16,56,640]{2,1,0:T(8,128)(2,1)} %shard_map.95), calls=%async_computation.1 | async-start | bytes 2293760 | tf_op jit(solution)/shard_map/all_to_all | solution.py:119
  99.9 0.0 copy-start.4
  99.9 18.0 %collective-permute-done.11.less_ref = bf16[4,8,32,512]{3,2,1,0:T(8,128)(2,1)} collective-permute-done((bf16[4,8,32,512]{3,2,1,0:T(8,128)(2,1)S(1)}, bf16[4,8,32,512]{3,2,1,0:T(8,128)(2,1)}, u32[]{:S(2)}, u32[]{:S(2)}) %collective-permute-start.11) | collective-permute-done | bytes 1048608 | tf_op jit(solution)/shard_map/ppermute | solution.py:164
  117.9 1.1 slice.47
  119.0 2.7 %collective-permute-start.13 = (bf16[4,8,16,512]{3,2,1,0:T(8,128)(2,1)S(1)}, bf16[4,8,16,512]{3,2,1,0:T(8,128)(2,1)}, u32[]{:S(2)}, u32[]{:S(2)}) collective-permute-start(bf16[4,8,16,512]{3,2,1,0:T(8,128)(2,1)S(1)} %slice.47), channel_id=1, source_target_pairs={{0,128},{128,256},{256,384},{384,0},{1,129},{129,257},{257,385},{3... | collective-permute-start | bytes 1572872 | tf_op jit(solution)/shard_map/ppermute | solution.py:164
  121.7 0.0 collective-permute-done.12.more_ref
  121.7 1.1 slice.48
  122.8 4.8 %collective-permute-start.14 = (bf16[4,8,16,512]{3,2,1,0:T(8,128)(2,1)S(1)}, bf16[4,8,16,512]{3,2,1,0:T(8,128)(2,1)S(1)}, u32[]{:S(2)}, u32[]{:S(2)}) collective-permute-start(bf16[4,8,16,512]{3,2,1,0:T(8,128)(2,1)S(1)} %slice.48), channel_id=1, source_target_pairs={{0,384},{128,0},{256,128},{384,256},{1,385},{129,1},{257,129},{385... | collective-permute-start | bytes 1572872 | tf_op jit(solution)/shard_map/ppermute | solution.py:164
  127.6 0.6 pad_add_fusion.2.place_ref
  128.3 0.7 maximum_maximum_fusion.stream_ref
  129.0 1.0 copy-done
  130.0 3.9 %shard_map.96 = bf16[56,512]{1,0:T(8,128)(2,1)} custom-call(bf16[16,56,640]{2,1,0:T(8,128)(2,1)} %copy-done), custom_call_target="tpu_custom_call" | custom-call | flops 2000000000 | bytes 1200000 | tf_op jit(solution)/shard_map/pallas_call | solution.py:109
  133.9 15.3 %all-gather = bf16[224,512]{1,0:T(8,128)(2,1)} all-gather(bf16[56,512]{1,0:T(8,128)(2,1)} %shard_map.96), channel_id=2, replica_groups=mesh['y'=4,'z'=8,'x'=4,'h'=2,'c'=2] {'h','c'}, dimensions={0}, use_global_device_ids=true | all-gather | bytes 286720 | tf_op jit(solution)/shard_map/all_gather | solution.py:213
  149.3 0.0 collective-permute-done.13.low_ref
  149.3 0.0 collective-permute-done.14.high_ref
  149.3 0.8 copy-done.7
  150.1 5.8 %shard_map.97 = (bf16[56,1024]{1,0:T(8,128)(2,1)}, f32[2,56,320]{2,1,0:T(8,128)}, bf16[2,56,320]{2,1,0:T(8,128)(2,1)}) custom-call(s32[4]{0:T(128)} %pad_add_fusion.2.place_ref, bf16[4,56,512]{2,1,0:T(8,128)(2,1)} %bitcast.38, bf16[4,8,32,512]{3,2,1,0:T(8,128)(2,1)} %copy-done.1, bf16[4,8,32,512]{3,2,1,0:T(8,128)(2,1)} %collective-permute-done.11.less_ref, ...), custom_call_target="tpu_custom_call" | custom-call | flops 4000000000 | bytes 7000000 | tf_op jit(solution)/shard_map/pallas_call | solution.py:150
  155.9 2.2 %collective-permute-start.15 = (bf16[2,56,320]{2,1,0:T(8,128)(2,1)}, bf16[2,56,320]{2,1,0:T(8,128)(2,1)S(1)}, u32[]{:S(2)}, u32[]{:S(2)}) collective-permute-start(bf16[2,56,320]{2,1,0:T(8,128)(2,1)} %get-tuple-element.7), channel_id=1, source_target_pairs={{0,1},{1,0},{2,3},{3,2},{4,5},{5,4},{6,7},{7,6},{8,9},{9,8},{10,11... | collective-permute-start | bytes 215048 | tf_op jit(solution)/shard_map/ppermute | solution.py:183
  158.2 0.1 slice_bitcast_fusion
  158.3 1.0 collective-permute-done.15
  159.3 0.9 convert_add_fusion
  160.3 5.0 %collective-permute-start.16 = (bf16[56,320]{1,0:T(8,128)(2,1)S(1)}, bf16[56,320]{1,0:T(8,128)(2,1)S(1)}, u32[]{:S(2)}, u32[]{:S(2)}) collective-permute-start(bf16[56,320]{1,0:T(8,128)(2,1)S(1)} %fusion.6), channel_id=1, source_target_pairs={{0,2},{2,0},{1,3},{3,1},{4,6},{6,4},{5,7},{7,5},{8,10},{10,8},{9,1... | collective-permute-start | bytes 107528 | tf_op jit(solution)/shard_map/ppermute | solution.py:183
  165.3 0.1 pad_add_fusion.1
  165.4 1.5 slice.39
  167.0 7.9 %collective-permute-done.16 = bf16[56,320]{1,0:T(8,128)(2,1)S(1)} collective-permute-done((bf16[56,320]{1,0:T(8,128)(2,1)S(1)}, bf16[56,320]{1,0:T(8,128)(2,1)S(1)}, u32[]{:S(2)}, u32[]{:S(2)}) %collective-permute-start.16) | collective-permute-done | bytes 35872 | tf_op jit(solution)/shard_map/ppermute | solution.py:183
  174.9 0.9 fusion
  (24 shorter events, 0.2 us)
Async XLA Ops:
  4.0 17.0 %collective-permute-start = (bf16[1,1536]{1,0:T(2,128)(2,1)S(1)}, bf16[1,1536]{1,0:T(2,128)(2,1)S(1)}, u32[]{:S(2)}, u32[]{:S(2)}) collective-permute-start(bf16[1,1536]{1,0:T(2,128)(2,1)S(1)} %fusion.9), channel_id=1, source_target_pairs={{0,4},{4,8},{8,12},{12,16},{16,20},{20,24},{24,28},{28,32},{32,36}... | collective-permute-start | bytes 9224 | tf_op jit(solution)/shard_map/ppermute | solution.py:199
  7.4 3.0 %collective-permute-start.4 = (bf16[32,512]{1,0:T(8,128)(2,1)}, bf16[32,512]{1,0:T(8,128)(2,1)S(1)}, u32[]{:S(2)}, u32[]{:S(2)}) collective-permute-start(bf16[32,512]{1,0:T(8,128)(2,1)} %bitcast.41), channel_id=1, source_target_pairs={{0,0},{1,128},{2,256},{3,384},{128,1},{129,129},{130,257},{131,385... | collective-permute-start | bytes 98312 | tf_op jit(solution)/shard_map/ppermute | solution.py:192
  10.3 10.7 %collective-permute-start.5 = (bf16[1,32,512]{2,1,0:T(8,128)(2,1)S(1)}, bf16[1,32,512]{2,1,0:T(8,128)(2,1)S(1)}, u32[]{:S(2)}, u32[]{:S(2)}) collective-permute-start(bf16[1,32,512]{2,1,0:T(8,128)(2,1)S(1)} %bitcast.31), channel_id=1, source_target_pairs={{0,64},{16,80},{32,96},{48,112},{64,0},{80,16},{96,32},{112,48},{1... | collective-permute-start | bytes 98312 | tf_op jit(solution)/shard_map/ppermute | solution.py:170
  15.0 42.4 %collective-permute-start.1 = (bf16[1,48,1024]{2,1,0:T(8,128)(2,1)S(1)}, bf16[1,48,1024]{2,1,0:T(8,128)(2,1)S(1)}, u32[]{:S(2)}, u32[]{:S(2)}) collective-permute-start(bf16[1,48,1024]{2,1,0:T(8,128)(2,1)S(1)} %maximum_bitcast_fusion), channel_id=1, source_target_pairs={{0,64},{16,80},{32,96},{48,112},{64,0},{80,16},{96,32},{112,48},{1... | collective-permute-start | bytes 294920 | tf_op jit(solution)/shard_map/ppermute | solution.py:170
  21.0 32.2 %collective-permute-start.6 = (bf16[2,32,512]{2,1,0:T(8,128)(2,1)S(1)}, bf16[2,32,512]{2,1,0:T(8,128)(2,1)S(1)}, u32[]{:S(2)}, u32[]{:S(2)}) collective-permute-start(bf16[2,32,512]{2,1,0:T(8,128)(2,1)S(1)} %pad_maximum_fusion.5), channel_id=1, source_target_pairs={{0,32},{16,48},{32,0},{48,16},{64,96},{80,112},{96,64},{112,80},{1... | collective-permute-start | bytes 196616 | tf_op jit(solution)/shard_map/ppermute | solution.py:170
  28.1 59.0 %all-to-all-start = ((bf16[16,56,512]{2,1,0:T(8,128)(2,1)}), bf16[16,56,512]{2,1,0:T(8,128)(2,1)S(1)}, u32[]{:S(2)}, u32[]{:S(2)}) async-start(bf16[16,56,512]{2,1,0:T(8,128)(2,1)} %broadcast_in_dim.36), calls=%async_computation | async-start | bytes 1835008 | tf_op jit(solution)/shard_map/all_to_all | solution.py:119
  53.2 8.1 %collective-permute-start.7 = (bf16[4,32,512]{2,1,0:T(8,128)(2,1)S(1)}, bf16[4,32,512]{2,1,0:T(8,128)(2,1)S(1)}, u32[]{:S(2)}, u32[]{:S(2)}) collective-permute-start(bf16[4,32,512]{2,1,0:T(8,128)(2,1)S(1)} %pad_maximum_fusion.4), channel_id=1, source_target_pairs={{0,16},{16,0},{32,48},{48,32},{64,80},{80,64},{96,112},{112,96},{1... | collective-permute-start | bytes 393224 | tf_op jit(solution)/shard_map/ppermute | solution.py:170
  57.5 14.2 %collective-permute-start.2 = (bf16[2,48,1024]{2,1,0:T(8,128)(2,1)S(1)}, bf16[2,48,1024]{2,1,0:T(8,128)(2,1)S(1)}, u32[]{:S(2)}, u32[]{:S(2)}) collective-permute-start(bf16[2,48,1024]{2,1,0:T(8,128)(2,1)S(1)} %pad_maximum_fusion.3), channel_id=1, source_target_pairs={{0,32},{16,48},{32,0},{48,16},{64,96},{80,112},{96,64},{112,80},{1... | collective-permute-start | bytes 589832 | tf_op jit(solution)/shard_map/ppermute | solution.py:170
  61.3 16.1 %collective-permute-start.10 = (bf16[8,32,512]{2,1,0:T(8,128)(2,1)S(1)}, bf16[8,32,512]{2,1,0:T(8,128)(2,1)S(1)}, u32[]{:S(2)}, u32[]{:S(2)}) collective-permute-start(bf16[8,32,512]{2,1,0:T(8,128)(2,1)S(1)} %get-tuple-element.9), channel_id=1, source_target_pairs={{0,12},{4,0},{8,4},{12,8},{1,13},{5,1},{9,5},{13,9},{2,14},{6,2},{... | collective-permute-start | bytes 786440 | tf_op jit(solution)/shard_map/ppermute | solution.py:164
  66.1 11.3 %collective-permute-start.9 = (bf16[8,32,512]{2,1,0:T(8,128)(2,1)S(1)}, bf16[8,32,512]{2,1,0:T(8,128)(2,1)S(1)}, u32[]{:S(2)}, u32[]{:S(2)}) collective-permute-start(bf16[8,32,512]{2,1,0:T(8,128)(2,1)S(1)} %get-tuple-element.9), channel_id=1, source_target_pairs={{0,8},{4,12},{8,0},{12,4},{1,9},{5,13},{9,1},{13,5},{2,10},{6,14},... | collective-permute-start | bytes 786440 | tf_op jit(solution)/shard_map/ppermute | solution.py:164
  68.9 10.9 %collective-permute-start.8 = (bf16[8,32,512]{2,1,0:T(8,128)(2,1)S(1)}, bf16[8,32,512]{2,1,0:T(8,128)(2,1)S(1)}, u32[]{:S(2)}, u32[]{:S(2)}) collective-permute-start(bf16[8,32,512]{2,1,0:T(8,128)(2,1)S(1)} %get-tuple-element.9), channel_id=1, source_target_pairs={{0,4},{4,8},{8,12},{12,0},{1,5},{5,9},{9,13},{13,1},{2,6},{6,10},{... | collective-permute-start | bytes 786440 | tf_op jit(solution)/shard_map/ppermute | solution.py:164
  71.8 15.3 %copy-start.3 = (bf16[4,48,1024]{2,1,0:T(8,128)(2,1)}, bf16[4,48,1024]{2,1,0:T(8,128)(2,1)S(1)}, u32[]{:S(2)}) copy-start(bf16[4,48,1024]{2,1,0:T(8,128)(2,1)S(1)} %pad_maximum_fusion.1.near_ref) | copy-start | bytes 1179652
  71.8 15.3 %collective-permute-start.3 = (bf16[4,48,1024]{2,1,0:T(8,128)(2,1)S(1)}, bf16[4,48,1024]{2,1,0:T(8,128)(2,1)}, u32[]{:S(2)}, u32[]{:S(2)}) collective-permute-start(bf16[4,48,1024]{2,1,0:T(8,128)(2,1)S(1)} %pad_maximum_fusion.1.near_ref), channel_id=1, source_target_pairs={{0,16},{16,0},{32,48},{48,32},{64,80},{80,64},{96,112},{112,96},{1... | collective-permute-start | bytes 1179656 | tf_op jit(solution)/shard_map/ppermute | solution.py:170
  80.0 16.2 %copy-start.1 = (bf16[4,8,32,512]{3,2,1,0:T(8,128)(2,1)}, bf16[4,8,32,512]{3,2,1,0:T(8,128)(2,1)S(1)}, u32[]{:S(2)}) copy-start(bf16[4,8,32,512]{3,2,1,0:T(8,128)(2,1)S(1)} %pad_maximum_fusion.own_ref) | copy-start | bytes 3145732
  80.0 38.0 %collective-permute-start.11 = (bf16[4,8,32,512]{3,2,1,0:T(8,128)(2,1)S(1)}, bf16[4,8,32,512]{3,2,1,0:T(8,128)(2,1)}, u32[]{:S(2)}, u32[]{:S(2)}) collective-permute-start(bf16[4,8,32,512]{3,2,1,0:T(8,128)(2,1)S(1)} %pad_maximum_fusion.own_ref), channel_id=1, source_target_pairs={{0,128},{128,256},{256,384},{384,0},{1,129},{129,257},{257,385},{3... | collective-permute-start | bytes 3145736 | tf_op jit(solution)/shard_map/ppermute | solution.py:164
  83.4 38.3 %collective-permute-start.12 = (bf16[4,8,32,512]{3,2,1,0:T(8,128)(2,1)S(1)}, bf16[4,8,32,512]{3,2,1,0:T(8,128)(2,1)}, u32[]{:S(2)}, u32[]{:S(2)}) collective-permute-start(bf16[4,8,32,512]{3,2,1,0:T(8,128)(2,1)S(1)} %pad_maximum_fusion.own_ref), channel_id=1, source_target_pairs={{0,384},{128,0},{256,128},{384,256},{1,385},{129,1},{257,129},{385... | collective-permute-start | bytes 3145736 | tf_op jit(solution)/shard_map/ppermute | solution.py:164
  87.1 1.0 copy-start.2
  96.2 32.8 %all-to-all-start.1 = ((bf16[16,56,640]{2,1,0:T(8,128)(2,1)}), bf16[16,56,640]{2,1,0:T(8,128)(2,1)S(1)}, u32[]{:S(2)}, u32[]{:S(2)}) async-start(bf16[16,56,640]{2,1,0:T(8,128)(2,1)} %shard_map.95), calls=%async_computation.1 | async-start | bytes 2293760 | tf_op jit(solution)/shard_map/all_to_all | solution.py:119
  99.9 28.4 %copy-start.4 = (bf16[48,1024]{1,0:T(8,128)(2,1)S(1)}, bf16[48,1024]{1,0:T(8,128)(2,1)}, u32[]{:S(2)}) copy-start(bf16[48,1024]{1,0:T(8,128)(2,1)} %param.11) | copy-start | bytes 294916
  119.0 30.3 %collective-permute-start.13 = (bf16[4,8,16,512]{3,2,1,0:T(8,128)(2,1)S(1)}, bf16[4,8,16,512]{3,2,1,0:T(8,128)(2,1)}, u32[]{:S(2)}, u32[]{:S(2)}) collective-permute-start(bf16[4,8,16,512]{3,2,1,0:T(8,128)(2,1)S(1)} %slice.47), channel_id=1, source_target_pairs={{0,128},{128,256},{256,384},{384,0},{1,129},{129,257},{257,385},{3... | collective-permute-start | bytes 1572872 | tf_op jit(solution)/shard_map/ppermute | solution.py:164
  122.8 26.5 %collective-permute-start.14 = (bf16[4,8,16,512]{3,2,1,0:T(8,128)(2,1)S(1)}, bf16[4,8,16,512]{3,2,1,0:T(8,128)(2,1)S(1)}, u32[]{:S(2)}, u32[]{:S(2)}) collective-permute-start(bf16[4,8,16,512]{3,2,1,0:T(8,128)(2,1)S(1)} %slice.48), channel_id=1, source_target_pairs={{0,384},{128,0},{256,128},{384,256},{1,385},{129,1},{257,129},{385... | collective-permute-start | bytes 1572872 | tf_op jit(solution)/shard_map/ppermute | solution.py:164
  129.0 1.0 copy-start
  149.3 0.8 copy-start.7
  150.1 8.1 %copy-start.6 = (s32[1,48]{1,0:T(1,128)S(1)}, s32[1,48]{1,0:T(1,128)}, u32[]{:S(2)}) copy-start(s32[1,48]{1,0:T(1,128)} %param.15) | copy-start | bytes 580
  150.1 24.8 %copy-start.5 = (bf16[192,320]{1,0:T(8,128)(2,1)S(1)}, bf16[192,320]{1,0:T(8,128)(2,1)}, u32[]{:S(2)}) copy-start(bf16[192,320]{1,0:T(8,128)(2,1)} %param.14) | copy-start | bytes 368644
  155.9 3.4 %collective-permute-start.15 = (bf16[2,56,320]{2,1,0:T(8,128)(2,1)}, bf16[2,56,320]{2,1,0:T(8,128)(2,1)S(1)}, u32[]{:S(2)}, u32[]{:S(2)}) collective-permute-start(bf16[2,56,320]{2,1,0:T(8,128)(2,1)} %get-tuple-element.7), channel_id=1, source_target_pairs={{0,1},{1,0},{2,3},{3,2},{4,5},{5,4},{6,7},{7,6},{8,9},{9,8},{10,11... | collective-permute-start | bytes 215048 | tf_op jit(solution)/shard_map/ppermute | solution.py:183
  160.3 14.6 %collective-permute-start.16 = (bf16[56,320]{1,0:T(8,128)(2,1)S(1)}, bf16[56,320]{1,0:T(8,128)(2,1)S(1)}, u32[]{:S(2)}, u32[]{:S(2)}) collective-permute-start(bf16[56,320]{1,0:T(8,128)(2,1)S(1)} %fusion.6), channel_id=1, source_target_pairs={{0,2},{2,0},{1,3},{3,1},{4,6},{6,4},{5,7},{7,5},{8,10},{10,8},{9,1... | collective-permute-start | bytes 107528 | tf_op jit(solution)/shard_map/ppermute | solution.py:183

commit v2 on v1

--- a/solution.py
+++ b/solution.py
@@ -5,6 +5,7 @@
 from jax.experimental.pallas import tpu as pltpu
 from jax.sharding import Mesh
 from jax.sharding import PartitionSpec as P
+
 
 DH = 128
 B_DEV = 192
@@ -20,12 +21,20 @@
 FAR = 1 << 30
 
 
-def pieces(value):
-    first = value.astype(jnp.bfloat16)
-    rest = value - first.astype(jnp.float32)
-    second = rest.astype(jnp.bfloat16)
-    third = (rest - second.astype(jnp.float32)).astype(jnp.bfloat16)
-    return [first, second, third]
+def prepare_kernel(starts_ref, keys_ref, values_ref, queries_ref, stream_ref, kv_ref, last_ref):
+    rows = keys_ref.shape[0]
+    valid = (starts_ref[...] < B_DEV).astype(jnp.float32)
+    count = jnp.sum(valid, axis=1, keepdims=True)
+    row = lax.broadcasted_iota(jnp.int32, (rows, rows), 0)
+    lane = lax.broadcasted_iota(jnp.int32, (rows, rows), 1)
+    held = jnp.sum(jnp.where(row == lane, valid, 0.0), axis=1, keepdims=True)
+    width = keys_ref.shape[1]
+    kv_ref[0, :, :width] = jnp.where(held > 0, keys_ref[...], jnp.full_like(keys_ref, MARK))
+    kv_ref[0, :, width:] = values_ref[...]
+    lane = lax.broadcasted_iota(jnp.int32, (1, rows), 1).astype(jnp.float32)
+    pick = (lane == count - 1).astype(jnp.bfloat16)
+    last_ref[:, :width] = jnp.dot(pick, queries_ref[...], preferred_element_type=jnp.float32).astype(jnp.bfloat16)
+    last_ref[:, width:] = jnp.dot(pick, stream_ref[...], preferred_element_type=jnp.float32).astype(jnp.bfloat16)
 
 
 def attend_kernel(place_ref, key_ids_ref, q_ref, near_ref, far_ref, out_ref):
@@ -53,13 +62,14 @@
             v = kv[:, width + h * DH : width + (h + 1) * DH]
             s = lax.dot_general(q, k, nt, preferred_element_type=jnp.float32) * (DH**-0.5)
             s = jnp.where(allowed, s, NEG)
-            peak = jnp.maximum(jnp.max(s, axis=1, keepdims=True), FLOOR)
+            peak = jnp.maximum(jnp.max(s, axis=1, keepdims=True), FLOOR).astype(jnp.bfloat16).astype(jnp.float32)
             e = jnp.exp(s - peak)
             total = jnp.sum(e, axis=1, keepdims=True)
             o = jnp.dot(e.astype(jnp.bfloat16), v, preferred_element_type=jnp.float32)
             out_ref[at_blocks, :, h * DH : (h + 1) * DH] = o.astype(jnp.bfloat16).reshape(group, rows, DH)
-            for at, part in enumerate(pieces(peak) + pieces(total)):
-                stats = jnp.where(lane == h * 6 + at, part.astype(jnp.float32), stats)
+            coarse = total.astype(jnp.bfloat16).astype(jnp.float32)
+            for at, part in enumerate((peak, coarse, total - coarse)):
+                stats = jnp.where(lane == h * 3 + at, part, stats)
         out_ref[at_blocks, :, width:] = stats.astype(jnp.bfloat16).reshape(group, rows, DH)
         return 0
 
@@ -69,28 +79,39 @@
 def combine_kernel(in_ref, out_ref):
     blocks, rows, width = in_ref.shape
     heads = (width - DH) // DH
+    stats = [in_ref[b, :, heads * DH :].astype(jnp.float32) for b in range(blocks)]
+    top = stats[0]
+    for b in range(1, blocks):
+        top = jnp.maximum(top, stats[b])
+    shares = [jnp.exp(jnp.minimum(stat - top, 0.0)) for stat in stats]
+    total = jnp.zeros_like(top)
+    for share, stat in zip(shares, stats):
+        total = total + share * (pltpu.roll(stat, DH - 1, 1) + pltpu.roll(stat, DH - 2, 1))
+    scale = 1.0 / jnp.where(total > 0, total, 1.0)
     for h in range(heads):
-        peaks, totals = [], []
-        for b in range(blocks):
-            stat = in_ref[b, :, heads * DH :].astype(jnp.float32)
-            at = h * 6
-            peaks.append(stat[:, at : at + 1] + stat[:, at + 1 : at + 2] + stat[:, at + 2 : at + 3])
-            totals.append(stat[:, at + 3 : at + 4] + stat[:, at + 4 : at + 5] + stat[:, at + 5 : at + 6])
-        top = peaks[0]
-        for b in range(1, blocks):
-            top = jnp.maximum(top, peaks[b])
-        total = jnp.zeros_like(top)
+        at = slice(h * DH, (h + 1) * DH)
         summed = jnp.zeros((rows, DH), jnp.float32)
         for b in range(blocks):
-            share = jnp.exp(peaks[b] - top)
-            total = total + share * totals[b]
-            summed = summed + share * in_ref[b, :, h * DH : (h + 1) * DH].astype(jnp.float32)
-        total = jnp.where(total > 0, total, 1.0)
-        out_ref[:, h * DH : (h + 1) * DH] = (summed / total).astype(jnp.bfloat16)
+            summed = summed + shares[b][:, h * 3 : h * 3 + 1] * in_ref[b, :, at].astype(jnp.float32)
+        out_ref[:, at] = (summed * scale[:, h * 3 : h * 3 + 1]).astype(jnp.bfloat16)
 
 
 VM = pl.BlockSpec(memory_space=pltpu.VMEM)
 SM = pl.BlockSpec(memory_space=pltpu.SMEM)
+
+
+def prepare(starts, keys, values, queries, stream):
+    rows, width = keys.shape
+    return pl.pallas_call(
+        prepare_kernel,
+        out_shape=(
+            jax.ShapeDtypeStruct((1, rows, 2 * width), jnp.bfloat16),
+            jax.ShapeDtypeStruct((1, width + stream.shape[1]), jnp.bfloat16),
+        ),
+        in_specs=[VM] * 5,
+        out_specs=(VM, VM),
+        cost_estimate=pl.CostEstimate(flops=1_000_000, bytes_accessed=400_000, transcendentals=0),
+    )(starts, keys, values, queries, stream)
 
 
 def attend(place, key_ids, q, near, far):
@@ -123,7 +144,7 @@
     return (distance & 1) * 4 + (distance & 2) + lax.div(distance, 4)
 
 
-def project_kernel(place_ref, attn_ref, own_ref, less_ref, more_ref, low_ref, high_ref, stream_ref, down_ref, new_ref, keep_ref, send_ref):
+def project_kernel(place_ref, attn_ref, own_ref, less_ref, more_ref, low_ref, high_ref, stream_ref, down_ref, out_ref, keep_ref, send_ref, new_ref):
     y, x, c, z = place_ref[0], place_ref[1], place_ref[2], place_ref[3]
     nt = (((1,), (1,)), ((), ()))
     span = 256
@@ -137,6 +158,7 @@
             weight = jnp.concatenate([ref[turn, spot] for turn, spot in spots for ref in refs], axis=0)
             mixed = mixed + lax.dot_general(attn, weight, nt, preferred_element_type=jnp.float32)
         new_ref[:, at * span : (at + 1) * span] = (total + mixed).astype(jnp.bfloat16)
+    out_ref[...] = new_ref[:ROWS]
     down = jnp.dot(new_ref[...], down_ref[...], preferred_element_type=jnp.float32)
     for half in range(2):
         at = half * 640
@@ -150,22 +172,42 @@
     return pl.pallas_call(
         project_kernel,
         out_shape=(
-            jax.ShapeDtypeStruct((rows, width), jnp.bfloat16),
+            jax.ShapeDtypeStruct((ROWS, width), jnp.bfloat16),
             jax.ShapeDtypeStruct((2, rows, 320), jnp.float32),
             jax.ShapeDtypeStruct((2, rows, 320), jnp.bfloat16),
         ),
         in_specs=[SM] + [VM] * 8,
         out_specs=(VM, VM, VM),
+        scratch_shapes=[pltpu.VMEM((rows, width), jnp.bfloat16)],
         cost_estimate=pl.CostEstimate(flops=4_000_000_000, bytes_accessed=7_000_000, transcendentals=0),
     )(place, attn, *weights, stream, down_weight)
 
 
+def owner_kernel(place_ref, keep_ref, arrived_ref, here_ref, there_ref):
+    first = keep_ref[0] + arrived_ref[0].astype(jnp.float32)
+    second = keep_ref[1] + arrived_ref[1].astype(jnp.float32)
+    near = place_ref[0] == 0
+    here_ref[...] = jnp.where(near, first, second)
+    there_ref[...] = jnp.where(near, second, first).astype(jnp.bfloat16)
+
+
+def owner(place, keep, arrived):
+    rows = keep.shape[1]
+    return pl.pallas_call(
+        owner_kernel,
+        out_shape=(jax.ShapeDtypeStruct((rows, 320), jnp.float32), jax.ShapeDtypeStruct((rows, 320), jnp.bfloat16)),
+        in_specs=[SM, VM, VM],
+        out_specs=(VM, VM),
+        cost_estimate=pl.CostEstimate(flops=1_000_000, bytes_accessed=900_000, transcendentals=0),
+    )(place, keep, arrived)
+
+
 def turned(value, axis, by):
     return lax.ppermute(value, axis, [(i, (i + by) % 4) for i in range(4)])
 
 
 def line_halves(block):
-    held = block[None]
+    held = block
     for bit in (4, 2, 1):
         other = lax.ppermute(held, "z", [(i, i ^ bit) for i in range(8)])
         if bit == 1:
@@ -186,18 +228,12 @@
 def on_device(queries, keys, values, patch_stream, out_weight, down_weight, byte_states, patch_starts):
     y, z, x, h, c = (lax.axis_index(a) for a in (*SEQ, *TP))
     starts = patch_starts.reshape(-1)
-    valid = starts < B_DEV
-    count = jnp.sum(valid.astype(jnp.int32))
     pairs = [(a * 4 + t, t * 4 + a) for a in range(4) for t in range(4)]
     block = lax.ppermute(out_weight.T, ("y", "h", "c"), pairs)
-    marked = jnp.where(valid[:, None], keys, jnp.bfloat16(MARK))
-    kv = jnp.concatenate([marked, values], axis=1)
-    blocks = jnp.concatenate(line_halves(block), axis=0)
-
-    last = lax.dynamic_slice(jnp.concatenate([queries, patch_stream], axis=1), (count - 1, 0), (1, 1536))
-    pairs = [(i, i + 1) for i in range(127)]
-    earlier = lax.ppermute(last, SEQ, pairs)
+    blocks = jnp.concatenate(line_halves(block[None]), axis=0)
     weights = plane_gathered(blocks)
+    kv, last = prepare(patch_starts, keys, values, queries, patch_stream)
+    earlier = lax.ppermute(last, SEQ, [(i, i + 1) for i in range(127)])
     near, far = line_halves(kv)
     q = jnp.concatenate([queries, earlier[:, :512], jnp.zeros((PAD - ROWS - 1, 512), jnp.bfloat16)], axis=0)
     stream = jnp.concatenate([patch_stream, earlier[:, 512:], jnp.zeros((PAD - ROWS - 1, 1024), jnp.bfloat16)], axis=0)
@@ -208,13 +244,13 @@
     away = slot // ROWS
     away = (away & 1) * 4 + (away & 2) + (away >> 2)
     key_ids = ((away ^ z) * (4 * ROWS) + slot % ROWS)[None]
-    attn = combine(exchange(attend(place, key_ids, q, near, far), PLANE))
+    parts = attend(place, key_ids, q, near, far)
+    parts = exchange(parts, PLANE)
+    attn = combine(parts)
 
     attn = lax.all_gather(attn, TP, axis=0)
-    new_rows, keep, send = project(jnp.stack([y, x, c, z]), attn, weights, stream, down_weight)
-    both = keep + across(send, "c").astype(jnp.float32)
-    here = jnp.where(h == 0, both[0], both[1])
-    there = jnp.where(h == 0, both[1], both[0]).astype(jnp.bfloat16)
+    new_patches, keep, send = project(jnp.stack([y, x, c, z]), attn, weights, stream, down_weight)
+    here, there = owner(h[None], keep, across(send, "c"))
     patch_down = (here + across(there, "h").astype(jnp.float32)).astype(jnp.bfloat16)
 
     position = jnp.arange(B_DEV, dtype=jnp.int32)[:, None]
@@ -223,7 +259,7 @@
     member = ((begins[None, :] <= position) & (position < ends[None, :])).astype(jnp.bfloat16)
     added = jnp.dot(member, patch_down, preferred_element_type=jnp.float32)
     new_bytes = (byte_states.astype(jnp.float32) + added).astype(jnp.bfloat16)
-    return (new_rows[:ROWS], new_bytes)
+    return (new_patches, new_bytes)
 
 
 def solution(mesh):

time: 177 us -> 178 us (level)
  the two profiles are of different devices: /device:TPU:128 before, /device:TPU:1 now
where the time goes in v2:
time: 178 us; the launch traced here: 177 us
  starting transfers between devices  77.8 us (44%)
  waiting for transfers between devices  44.6 us (25%)
  blocking collectives  20.9 us (12%)
  Pallas kernels  19.8 us (11%)
  local copies, waits for them, and re-layouts  7.69 us (4%)
  other arithmetic  3.72 us (2%)
    ppermute x7, starting transfers between devices, turned(): return lax.ppermute(value, axis, [(i, (i + by) % 4) for i in range(4)])  22.8 us
    ppermute x7, waiting for transfers between devices, turned(): return lax.ppermute(value, axis, [(i, (i + by) % 4) for i in range(4)])  22.3 us
    ppermute x6, starting transfers between devices, line_halves(): other = lax.ppermute(held, 'z', [(i, i ^ bit) for i in range(8)])  22.2 us
    all_gather x1, blocking collectives, on_device(): attn = lax.all_gather(attn, TP, axis=0)  20.9 us
    all_to_all x2, starting transfers between devices, exchange(): return lax.all_to_all(value, axes, split_axis=0, concat_axis=0, tiled=True)  20.1 us
    ppermute x2, waiting for transfers between devices, across(): return lax.ppermute(value, axis, [(0, 1), (1, 0)])  11.9 us
    ppermute x6, waiting for transfers between devices, line_halves(): other = lax.ppermute(held, 'z', [(i, i ^ bit) for i in range(8)])  10.4 us
    pallas_call x1, Pallas kernels, attend(): pl.pallas_call(attend_kernel, out_shape=jax.ShapeDtypeStruct((blocks, row...  7.92 us
  transfers between devices with their start and end apart: 19, of which 5 were waited for; matrix products, arithmetic and copies ran while one was open for 4% of the time, Pallas kernels for 7%

profile of v2, /device:TPU:1, one launch (start us, length us, event | category | flops | bytes accessed | tf_op | source)
XLA Modules:
  0.0 177.1 jit_solution(15940847022362143309)
XLA Ops:
  0.6 4.6 %collective-permute-start.4 = (bf16[32,512]{1,0:T(8,128)(2,1)}, bf16[32,512]{1,0:T(8,128)(2,1)S(1)}, u32[]{:S(2)}, u32[]{:S(2)}) collective-permute-start(bf16[32,512]{1,0:T(8,128)(2,1)} %bitcast.30), channel_id=1, source_target_pairs={{0,0},{1,128},{2,256},{3,384},{128,1},{129,129},{130,257},{131,385... | collective-permute-start | bytes 98312 | tf_op jit(solution)/shard_map/ppermute | solution.py:232
  5.2 1.8 %shard_map.95 = (bf16[1,48,1024]{2,1,0:T(8,128)(2,1)}, bf16[1,1536]{1,0:T(2,128)(2,1)}) custom-call(s32[1,48]{1,0:T(1,128)} %starts_ref.1, bf16[48,512]{1,0:T(8,128)(2,1)} %keys_ref.1, bf16[48,512]{1,0:T(8,128)(2,1)} %values_ref.1, bf16[48,512]{1,0:T(8,128)(2,1)} %queries_ref.1, bf16[48,1024]{1,0:T(8,128)(2,1)} %stream_ref.1), custom_call_target="tpu_custom_call" | custom-call | flops 1000000 | bytes 400000 | tf_op jit(solution)/shard_map/pallas_call | solution.py:105
  7.0 3.1 %collective-permute-start = (bf16[1,1536]{1,0:T(2,128)(2,1)}, bf16[1,1536]{1,0:T(2,128)(2,1)S(1)}, u32[]{:S(2)}, u32[]{:S(2)}) collective-permute-start(bf16[1,1536]{1,0:T(2,128)(2,1)} %get-tuple-element.9), channel_id=1, source_target_pairs={{0,4},{4,8},{8,12},{12,16},{16,20},{20,24},{24,28},{28,32},{32,36}... | collective-permute-start | bytes 9224 | tf_op jit(solution)/shard_map/ppermute | solution.py:236
  10.1 8.8 %collective-permute-start.1 = (bf16[1,48,1024]{2,1,0:T(8,128)(2,1)}, bf16[1,48,1024]{2,1,0:T(8,128)(2,1)S(1)}, u32[]{:S(2)}, u32[]{:S(2)}) collective-permute-start(bf16[1,48,1024]{2,1,0:T(8,128)(2,1)} %get-tuple-element.10), channel_id=1, source_target_pairs={{0,64},{16,80},{32,96},{48,112},{64,0},{80,16},{96,32},{112,48},{1... | collective-permute-start | bytes 294920 | tf_op jit(solution)/shard_map/ppermute | solution.py:212
  19.0 0.0 collective-permute-done.4
  19.0 1.9 %collective-permute-start.5 = (bf16[1,32,512]{2,1,0:T(8,128)(2,1)S(1)}, bf16[1,32,512]{2,1,0:T(8,128)(2,1)S(1)}, u32[]{:S(2)}, u32[]{:S(2)}) collective-permute-start(bf16[1,32,512]{2,1,0:T(8,128)(2,1)S(1)} %bitcast.20), channel_id=1, source_target_pairs={{0,64},{16,80},{32,96},{48,112},{64,0},{80,16},{96,32},{112,48},{1... | collective-permute-start | bytes 98312 | tf_op jit(solution)/shard_map/ppermute | solution.py:212
  20.9 0.9 constant_dynamic-update-slice_fusion.2
  21.8 0.1 pad.27.clone
  21.9 0.0 collective-permute-done
  21.9 10.4 %collective-permute-done.5 = bf16[1,32,512]{2,1,0:T(8,128)(2,1)S(1)} collective-permute-done((bf16[1,32,512]{2,1,0:T(8,128)(2,1)S(1)}, bf16[1,32,512]{2,1,0:T(8,128)(2,1)S(1)}, u32[]{:S(2)}, u32[]{:S(2)}) %collective-permute-start.5) | collective-permute-done | bytes 32800 | tf_op jit(solution)/shard_map/ppermute | solution.py:212
  32.3 1.9 %collective-permute-start.6 = (bf16[2,32,512]{2,1,0:T(8,128)(2,1)S(1)}, bf16[2,32,512]{2,1,0:T(8,128)(2,1)S(1)}, u32[]{:S(2)}, u32[]{:S(2)}) collective-permute-start(bf16[2,32,512]{2,1,0:T(8,128)(2,1)S(1)} %pad_maximum_fusion.4), channel_id=1, source_target_pairs={{0,32},{16,48},{32,0},{48,16},{64,96},{80,112},{96,64},{112,80},{1... | collective-permute-start | bytes 196616 | tf_op jit(solution)/shard_map/ppermute | solution.py:212
  34.2 0.9 maximum_maximum_fusion.1
  35.1 1.0 broadcast_in_dim.11
  36.1 16.4 %all-to-all-start = ((bf16[16,56,512]{2,1,0:T(8,128)(2,1)}), bf16[16,56,512]{2,1,0:T(8,128)(2,1)S(1)}, u32[]{:S(2)}, u32[]{:S(2)}) async-start(bf16[16,56,512]{2,1,0:T(8,128)(2,1)} %broadcast_in_dim.11), calls=%async_computation | async-start | bytes 1835008 | tf_op jit(solution)/shard_map/all_to_all | solution.py:140
  52.6 0.0 collective-permute-done.6
  52.6 1.9 %collective-permute-start.7 = (bf16[4,32,512]{2,1,0:T(8,128)(2,1)S(1)}, bf16[4,32,512]{2,1,0:T(8,128)(2,1)S(1)}, u32[]{:S(2)}, u32[]{:S(2)}) collective-permute-start(bf16[4,32,512]{2,1,0:T(8,128)(2,1)S(1)} %pad_maximum_fusion.3), channel_id=1, source_target_pairs={{0,16},{16,0},{32,48},{48,32},{64,80},{80,64},{96,112},{112,96},{1... | collective-permute-start | bytes 393224 | tf_op jit(solution)/shard_map/ppermute | solution.py:212
  54.5 0.0 collective-permute-done.1
  54.6 4.3 %collective-permute-start.2 = (bf16[2,48,1024]{2,1,0:T(8,128)(2,1)S(1)}, bf16[2,48,1024]{2,1,0:T(8,128)(2,1)S(1)}, u32[]{:S(2)}, u32[]{:S(2)}) collective-permute-start(bf16[2,48,1024]{2,1,0:T(8,128)(2,1)S(1)} %pad_maximum_fusion.2), channel_id=1, source_target_pairs={{0,32},{16,48},{32,0},{48,16},{64,96},{80,112},{96,64},{112,80},{1... | collective-permute-start | bytes 589832 | tf_op jit(solution)/shard_map/ppermute | solution.py:212
  58.9 0.0 collective-permute-done.7
  58.9 4.5 %collective-permute-start.10 = (bf16[8,32,512]{2,1,0:T(8,128)(2,1)S(1)}, bf16[8,32,512]{2,1,0:T(8,128)(2,1)S(1)}, u32[]{:S(2)}, u32[]{:S(2)}) collective-permute-start(bf16[8,32,512]{2,1,0:T(8,128)(2,1)S(1)} %get-tuple-element.17), channel_id=1, source_target_pairs={{0,12},{4,0},{8,4},{12,8},{1,13},{5,1},{9,5},{13,9},{2,14},{6,2},{... | collective-permute-start | bytes 786440 | tf_op jit(solution)/shard_map/ppermute | solution.py:206
  63.4 2.5 %collective-permute-start.9 = (bf16[8,32,512]{2,1,0:T(8,128)(2,1)S(1)}, bf16[8,32,512]{2,1,0:T(8,128)(2,1)S(1)}, u32[]{:S(2)}, u32[]{:S(2)}) collective-permute-start(bf16[8,32,512]{2,1,0:T(8,128)(2,1)S(1)} %get-tuple-element.17), channel_id=1, source_target_pairs={{0,8},{4,12},{8,0},{12,4},{1,9},{5,13},{9,1},{13,5},{2,10},{6,14},... | collective-permute-start | bytes 786440 | tf_op jit(solution)/shard_map/ppermute | solution.py:206
  65.9 2.5 %collective-permute-start.8 = (bf16[8,32,512]{2,1,0:T(8,128)(2,1)S(1)}, bf16[8,32,512]{2,1,0:T(8,128)(2,1)S(1)}, u32[]{:S(2)}, u32[]{:S(2)}) collective-permute-start(bf16[8,32,512]{2,1,0:T(8,128)(2,1)S(1)} %get-tuple-element.17), channel_id=1, source_target_pairs={{0,4},{4,8},{8,12},{12,0},{1,5},{5,9},{9,13},{13,1},{2,6},{6,10},{... | collective-permute-start | bytes 786440 | tf_op jit(solution)/shard_map/ppermute | solution.py:206
  68.4 0.0 collective-permute-done.2
  68.4 3.4 %collective-permute-start.3 = (bf16[4,48,1024]{2,1,0:T(8,128)(2,1)S(1)}, bf16[4,48,1024]{2,1,0:T(8,128)(2,1)}, u32[]{:S(2)}, u32[]{:S(2)}) collective-permute-start(bf16[4,48,1024]{2,1,0:T(8,128)(2,1)S(1)} %constant_dynamic-update-slice_fusion.near_ref), channel_id=1, source_target_pairs={{0,16},{16,0},{32,48},{48,32},{64,80},{80,64},{96,112},{112,96},{1... | collective-permute-start | bytes 1179656 | tf_op jit(solution)/shard_map/ppermute | solution.py:212
  71.8 0.6 pad_add_fusion.3.place_ref
  72.4 0.6 fusion.5.key_ids_ref
  73.0 0.0 collective-permute-done.10
  73.0 0.0 collective-permute-done.9
  73.0 6.9 %collective-permute-done.8 = bf16[8,32,512]{2,1,0:T(8,128)(2,1)S(1)} collective-permute-done((bf16[8,32,512]{2,1,0:T(8,128)(2,1)S(1)}, bf16[8,32,512]{2,1,0:T(8,128)(2,1)S(1)}, u32[]{:S(2)}, u32[]{:S(2)}) %collective-permute-start.8) | collective-permute-done | bytes 262176 | tf_op jit(solution)/shard_map/ppermute | solution.py:206
  79.9 0.1 pad_maximum_fusion.own_ref
  80.0 0.0 copy-start.1
  80.1 3.1 %collective-permute-start.11 = (bf16[4,8,32,512]{3,2,1,0:T(8,128)(2,1)S(1)}, bf16[4,8,32,512]{3,2,1,0:T(8,128)(2,1)}, u32[]{:S(2)}, u32[]{:S(2)}) collective-permute-start(bf16[4,8,32,512]{3,2,1,0:T(8,128)(2,1)S(1)} %pad_maximum_fusion.own_ref), channel_id=1, source_target_pairs={{0,128},{128,256},{256,384},{384,0},{1,129},{129,257},{257,385},{3... | collective-permute-start | bytes 3145736 | tf_op jit(solution)/shard_map/ppermute | solution.py:206
  83.2 3.4 %collective-permute-start.12 = (bf16[4,8,32,512]{3,2,1,0:T(8,128)(2,1)S(1)}, bf16[4,8,32,512]{3,2,1,0:T(8,128)(2,1)}, u32[]{:S(2)}, u32[]{:S(2)}) collective-permute-start(bf16[4,8,32,512]{3,2,1,0:T(8,128)(2,1)S(1)} %pad_maximum_fusion.own_ref), channel_id=1, source_target_pairs={{0,384},{128,0},{256,128},{384,256},{1,385},{129,1},{257,129},{385... | collective-permute-start | bytes 3145736 | tf_op jit(solution)/shard_map/ppermute | solution.py:206
  86.6 0.0 collective-permute-done.3.far_ref
  86.6 0.0 all-to-all-done.q_ref
  86.6 1.0 copy-done.2
  87.6 7.9 %shard_map.96 = bf16[16,56,640]{2,1,0:T(8,128)(2,1)} custom-call(s32[2]{0:T(128)} %pad_add_fusion.3.place_ref, s32[1,384]{1,0:T(1,128)} %fusion.5.key_ids_ref, bf16[16,56,512]{2,1,0:T(8,128)(2,1)} %copy-done.2, bf16[4,48,1024]{2,1,0:T(8,128)(2,1)} %copy-done.7, bf16[4,48,1024]{2,1,0:T(8,128)(2,1)} %collective-permute-done.3.far_ref), custom_call_target="tpu_custom_call" | custom-call | flops 4000000000 | bytes 3000000 | tf_op jit(solution)/shard_map/pallas_call | solution.py:119
  95.5 3.7 %all-to-all-start.1 = ((bf16[16,56,640]{2,1,0:T(8,128)(2,1)}), bf16[16,56,640]{2,1,0:T(8,128)(2,1)S(1)}, u32[]{:S(2)}, u32[]{:S(2)}) async-start(bf16[16,56,640]{2,1,0:T(8,128)(2,1)} %shard_map.96), calls=%async_computation.1 | async-start | bytes 2293760 | tf_op jit(solution)/shard_map/all_to_all | solution.py:140
  99.2 0.0 copy-start.3
  99.2 15.3 %collective-permute-done.11.less_ref = bf16[4,8,32,512]{3,2,1,0:T(8,128)(2,1)} collective-permute-done((bf16[4,8,32,512]{3,2,1,0:T(8,128)(2,1)S(1)}, bf16[4,8,32,512]{3,2,1,0:T(8,128)(2,1)}, u32[]{:S(2)}, u32[]{:S(2)}) %collective-permute-start.11) | collective-permute-done | bytes 1048608 | tf_op jit(solution)/shard_map/ppermute | solution.py:206
  114.6 1.1 slice.33
  115.6 2.5 %collective-permute-start.13 = (bf16[4,8,16,512]{3,2,1,0:T(8,128)(2,1)S(1)}, bf16[4,8,16,512]{3,2,1,0:T(8,128)(2,1)}, u32[]{:S(2)}, u32[]{:S(2)}) collective-permute-start(bf16[4,8,16,512]{3,2,1,0:T(8,128)(2,1)S(1)} %slice.33), channel_id=1, source_target_pairs={{0,128},{128,256},{256,384},{384,0},{1,129},{129,257},{257,385},{3... | collective-permute-start | bytes 1572872 | tf_op jit(solution)/shard_map/ppermute | solution.py:206
  118.2 0.0 collective-permute-done.12.more_ref
  118.2 1.1 slice.34
  119.3 4.3 %collective-permute-start.14 = (bf16[4,8,16,512]{3,2,1,0:T(8,128)(2,1)S(1)}, bf16[4,8,16,512]{3,2,1,0:T(8,128)(2,1)S(1)}, u32[]{:S(2)}, u32[]{:S(2)}) collective-permute-start(bf16[4,8,16,512]{3,2,1,0:T(8,128)(2,1)S(1)} %slice.34), channel_id=1, source_target_pairs={{0,384},{128,0},{256,128},{384,256},{1,385},{129,1},{257,129},{385... | collective-permute-start | bytes 1572872 | tf_op jit(solution)/shard_map/ppermute | solution.py:206
  123.6 0.6 pad_add_fusion.2.place_ref
  124.2 0.7 maximum_maximum_fusion.stream_ref
  124.9 0.0 all-to-all-done.1.in_ref
  124.9 1.0 copy-done
  125.9 2.6 %shard_map.97 = bf16[56,512]{1,0:T(8,128)(2,1)} custom-call(bf16[16,56,640]{2,1,0:T(8,128)(2,1)} %copy-done), custom_call_target="tpu_custom_call" | custom-call | flops 2000000000 | bytes 1200000 | tf_op jit(solution)/shard_map/pallas_call | solution.py:130
  128.5 20.9 %all-gather = bf16[224,512]{1,0:T(8,128)(2,1)} all-gather(bf16[56,512]{1,0:T(8,128)(2,1)} %shard_map.97), channel_id=2, replica_groups=mesh['y'=4,'z'=8,'x'=4,'h'=2,'c'=2] {'h','c'}, dimensions={0}, use_global_device_ids=true | all-gather | bytes 286720 | tf_op jit(solution)/shard_map/all_gather | solution.py:251
  149.4 0.0 collective-permute-done.13.low_ref
  149.4 0.0 collective-permute-done.14.high_ref
  149.4 0.8 copy-done.9
  150.2 5.8 %shard_map.98 = (bf16[48,1024]{1,0:T(8,128)(2,1)}, f32[2,56,320]{2,1,0:T(8,128)}, bf16[2,56,320]{2,1,0:T(8,128)(2,1)}) custom-call(s32[4]{0:T(128)} %pad_add_fusion.2.place_ref, bf16[4,56,512]{2,1,0:T(8,128)(2,1)} %bitcast.27, bf16[4,8,32,512]{3,2,1,0:T(8,128)(2,1)} %copy-done.1, bf16[4,8,32,512]{3,2,1,0:T(8,128)(2,1)} %collective-permute-done.11.less_ref, ...), custom_call_target="tpu_custom_call" | custom-call | flops 4000000000 | bytes 7000000 | tf_op jit(solution)/shard_map/pallas_call | solution.py:172
  156.0 2.1 %collective-permute-start.15 = (bf16[2,56,320]{2,1,0:T(8,128)(2,1)}, bf16[2,56,320]{2,1,0:T(8,128)(2,1)S(1)}, u32[]{:S(2)}, u32[]{:S(2)}) collective-permute-start(bf16[2,56,320]{2,1,0:T(8,128)(2,1)} %get-tuple-element.13), channel_id=1, source_target_pairs={{0,1},{1,0},{2,3},{3,2},{4,5},{5,4},{6,7},{7,6},{8,9},{9,8},{10,11... | collective-permute-start | bytes 215048 | tf_op jit(solution)/shard_map/ppermute | solution.py:225
  158.1 0.1 slice_bitcast_fusion
  158.2 1.2 collective-permute-done.15.arrived_ref
  159.4 0.6 copy-done.6
  160.1 1.6 shard_map.99
  161.7 2.9 %collective-permute-start.16 = (bf16[56,320]{1,0:T(8,128)(2,1)}, bf16[56,320]{1,0:T(8,128)(2,1)S(1)}, u32[]{:S(2)}, u32[]{:S(2)}) collective-permute-start(bf16[56,320]{1,0:T(8,128)(2,1)} %get-tuple-element.15), channel_id=1, source_target_pairs={{0,2},{2,0},{1,3},{3,1},{4,6},{6,4},{5,7},{7,5},{8,10},{10,8},{9,1... | collective-permute-start | bytes 107528 | tf_op jit(solution)/shard_map/ppermute | solution.py:225
  164.6 0.1 pad_add_fusion.1
  164.7 10.7 %collective-permute-done.16 = bf16[56,320]{1,0:T(8,128)(2,1)S(1)} collective-permute-done((bf16[56,320]{1,0:T(8,128)(2,1)}, bf16[56,320]{1,0:T(8,128)(2,1)S(1)}, u32[]{:S(2)}, u32[]{:S(2)}) %collective-permute-start.16) | collective-permute-done | bytes 35872 | tf_op jit(solution)/shard_map/ppermute | solution.py:225
  175.4 1.7 fusion
  (24 shorter events, 0.2 us)
Async XLA Ops:
  0.6 18.3 %collective-permute-start.4 = (bf16[32,512]{1,0:T(8,128)(2,1)}, bf16[32,512]{1,0:T(8,128)(2,1)S(1)}, u32[]{:S(2)}, u32[]{:S(2)}) collective-permute-start(bf16[32,512]{1,0:T(8,128)(2,1)} %bitcast.30), channel_id=1, source_target_pairs={{0,0},{1,128},{2,256},{3,384},{128,1},{129,129},{130,257},{131,385... | collective-permute-start | bytes 98312 | tf_op jit(solution)/shard_map/ppermute | solution.py:232
  7.0 14.9 %collective-permute-start = (bf16[1,1536]{1,0:T(2,128)(2,1)}, bf16[1,1536]{1,0:T(2,128)(2,1)S(1)}, u32[]{:S(2)}, u32[]{:S(2)}) collective-permute-start(bf16[1,1536]{1,0:T(2,128)(2,1)} %get-tuple-element.9), channel_id=1, source_target_pairs={{0,4},{4,8},{8,12},{12,16},{16,20},{20,24},{24,28},{28,32},{32,36}... | collective-permute-start | bytes 9224 | tf_op jit(solution)/shard_map/ppermute | solution.py:236
  10.1 44.4 %collective-permute-start.1 = (bf16[1,48,1024]{2,1,0:T(8,128)(2,1)}, bf16[1,48,1024]{2,1,0:T(8,128)(2,1)S(1)}, u32[]{:S(2)}, u32[]{:S(2)}) collective-permute-start(bf16[1,48,1024]{2,1,0:T(8,128)(2,1)} %get-tuple-element.10), channel_id=1, source_target_pairs={{0,64},{16,80},{32,96},{48,112},{64,0},{80,16},{96,32},{112,48},{1... | collective-permute-start | bytes 294920 | tf_op jit(solution)/shard_map/ppermute | solution.py:212
  19.0 13.3 %collective-permute-start.5 = (bf16[1,32,512]{2,1,0:T(8,128)(2,1)S(1)}, bf16[1,32,512]{2,1,0:T(8,128)(2,1)S(1)}, u32[]{:S(2)}, u32[]{:S(2)}) collective-permute-start(bf16[1,32,512]{2,1,0:T(8,128)(2,1)S(1)} %bitcast.20), channel_id=1, source_target_pairs={{0,64},{16,80},{32,96},{48,112},{64,0},{80,16},{96,32},{112,48},{1... | collective-permute-start | bytes 98312 | tf_op jit(solution)/shard_map/ppermute | solution.py:212
  32.3 20.3 %collective-permute-start.6 = (bf16[2,32,512]{2,1,0:T(8,128)(2,1)S(1)}, bf16[2,32,512]{2,1,0:T(8,128)(2,1)S(1)}, u32[]{:S(2)}, u32[]{:S(2)}) collective-permute-start(bf16[2,32,512]{2,1,0:T(8,128)(2,1)S(1)} %pad_maximum_fusion.4), channel_id=1, source_target_pairs={{0,32},{16,48},{32,0},{48,16},{64,96},{80,112},{96,64},{112,80},{1... | collective-permute-start | bytes 196616 | tf_op jit(solution)/shard_map/ppermute | solution.py:212
  36.1 18.4 %copy-start.4 = (bf16[1,48,1024]{2,1,0:T(8,128)(2,1)S(1)}, bf16[1,48,1024]{2,1,0:T(8,128)(2,1)}, u32[]{:S(2)}) copy-start(bf16[1,48,1024]{2,1,0:T(8,128)(2,1)} %get-tuple-element.10) | copy-start | bytes 294916
  36.1 50.5 %all-to-all-start = ((bf16[16,56,512]{2,1,0:T(8,128)(2,1)}), bf16[16,56,512]{2,1,0:T(8,128)(2,1)S(1)}, u32[]{:S(2)}, u32[]{:S(2)}) async-start(bf16[16,56,512]{2,1,0:T(8,128)(2,1)} %broadcast_in_dim.11), calls=%async_computation | async-start | bytes 1835008 | tf_op jit(solution)/shard_map/all_to_all | solution.py:140
  52.6 6.3 %collective-permute-start.7 = (bf16[4,32,512]{2,1,0:T(8,128)(2,1)S(1)}, bf16[4,32,512]{2,1,0:T(8,128)(2,1)S(1)}, u32[]{:S(2)}, u32[]{:S(2)}) collective-permute-start(bf16[4,32,512]{2,1,0:T(8,128)(2,1)S(1)} %pad_maximum_fusion.3), channel_id=1, source_target_pairs={{0,16},{16,0},{32,48},{48,32},{64,80},{80,64},{96,112},{112,96},{1... | collective-permute-start | bytes 393224 | tf_op jit(solution)/shard_map/ppermute | solution.py:212
  54.6 13.8 %collective-permute-start.2 = (bf16[2,48,1024]{2,1,0:T(8,128)(2,1)S(1)}, bf16[2,48,1024]{2,1,0:T(8,128)(2,1)S(1)}, u32[]{:S(2)}, u32[]{:S(2)}) collective-permute-start(bf16[2,48,1024]{2,1,0:T(8,128)(2,1)S(1)} %pad_maximum_fusion.2), channel_id=1, source_target_pairs={{0,32},{16,48},{32,0},{48,16},{64,96},{80,112},{96,64},{112,80},{1... | collective-permute-start | bytes 589832 | tf_op jit(solution)/shard_map/ppermute | solution.py:212
  58.9 14.1 %collective-permute-start.10 = (bf16[8,32,512]{2,1,0:T(8,128)(2,1)S(1)}, bf16[8,32,512]{2,1,0:T(8,128)(2,1)S(1)}, u32[]{:S(2)}, u32[]{:S(2)}) collective-permute-start(bf16[8,32,512]{2,1,0:T(8,128)(2,1)S(1)} %get-tuple-element.17), channel_id=1, source_target_pairs={{0,12},{4,0},{8,4},{12,8},{1,13},{5,1},{9,5},{13,9},{2,14},{6,2},{... | collective-permute-start | bytes 786440 | tf_op jit(solution)/shard_map/ppermute | solution.py:206
  63.4 9.6 %collective-permute-start.9 = (bf16[8,32,512]{2,1,0:T(8,128)(2,1)S(1)}, bf16[8,32,512]{2,1,0:T(8,128)(2,1)S(1)}, u32[]{:S(2)}, u32[]{:S(2)}) collective-permute-start(bf16[8,32,512]{2,1,0:T(8,128)(2,1)S(1)} %get-tuple-element.17), channel_id=1, source_target_pairs={{0,8},{4,12},{8,0},{12,4},{1,9},{5,13},{9,1},{13,5},{2,10},{6,14},... | collective-permute-start | bytes 786440 | tf_op jit(solution)/shard_map/ppermute | solution.py:206
  65.9 14.0 %collective-permute-start.8 = (bf16[8,32,512]{2,1,0:T(8,128)(2,1)S(1)}, bf16[8,32,512]{2,1,0:T(8,128)(2,1)S(1)}, u32[]{:S(2)}, u32[]{:S(2)}) collective-permute-start(bf16[8,32,512]{2,1,0:T(8,128)(2,1)S(1)} %get-tuple-element.17), channel_id=1, source_target_pairs={{0,4},{4,8},{8,12},{12,0},{1,5},{5,9},{9,13},{13,1},{2,6},{6,10},{... | collective-permute-start | bytes 786440 | tf_op jit(solution)/shard_map/ppermute | solution.py:206
  68.4 18.2 %copy-start.7 = (bf16[4,48,1024]{2,1,0:T(8,128)(2,1)}, bf16[4,48,1024]{2,1,0:T(8,128)(2,1)S(1)}, u32[]{:S(2)}) copy-start(bf16[4,48,1024]{2,1,0:T(8,128)(2,1)S(1)} %constant_dynamic-update-slice_fusion.near_ref) | copy-start | bytes 1179652
  68.4 18.1 %collective-permute-start.3 = (bf16[4,48,1024]{2,1,0:T(8,128)(2,1)S(1)}, bf16[4,48,1024]{2,1,0:T(8,128)(2,1)}, u32[]{:S(2)}, u32[]{:S(2)}) collective-permute-start(bf16[4,48,1024]{2,1,0:T(8,128)(2,1)S(1)} %constant_dynamic-update-slice_fusion.near_ref), channel_id=1, source_target_pairs={{0,16},{16,0},{32,48},{48,32},{64,80},{80,64},{96,112},{112,96},{1... | collective-permute-start | bytes 1179656 | tf_op jit(solution)/shard_map/ppermute | solution.py:212
  80.0 15.5 %copy-start.1 = (bf16[4,8,32,512]{3,2,1,0:T(8,128)(2,1)}, bf16[4,8,32,512]{3,2,1,0:T(8,128)(2,1)S(1)}, u32[]{:S(2)}) copy-start(bf16[4,8,32,512]{3,2,1,0:T(8,128)(2,1)S(1)} %pad_maximum_fusion.own_ref) | copy-start | bytes 3145732
  80.1 34.5 %collective-permute-start.11 = (bf16[4,8,32,512]{3,2,1,0:T(8,128)(2,1)S(1)}, bf16[4,8,32,512]{3,2,1,0:T(8,128)(2,1)}, u32[]{:S(2)}, u32[]{:S(2)}) collective-permute-start(bf16[4,8,32,512]{3,2,1,0:T(8,128)(2,1)S(1)} %pad_maximum_fusion.own_ref), channel_id=1, source_target_pairs={{0,128},{128,256},{256,384},{384,0},{1,129},{129,257},{257,385},{3... | collective-permute-start | bytes 3145736 | tf_op jit(solution)/shard_map/ppermute | solution.py:206
  83.2 35.0 %collective-permute-start.12 = (bf16[4,8,32,512]{3,2,1,0:T(8,128)(2,1)S(1)}, bf16[4,8,32,512]{3,2,1,0:T(8,128)(2,1)}, u32[]{:S(2)}, u32[]{:S(2)}) collective-permute-start(bf16[4,8,32,512]{3,2,1,0:T(8,128)(2,1)S(1)} %pad_maximum_fusion.own_ref), channel_id=1, source_target_pairs={{0,384},{128,0},{256,128},{384,256},{1,385},{129,1},{257,129},{385... | collective-permute-start | bytes 3145736 | tf_op jit(solution)/shard_map/ppermute | solution.py:206
  86.6 1.0 copy-start.2
  95.5 29.4 %all-to-all-start.1 = ((bf16[16,56,640]{2,1,0:T(8,128)(2,1)}), bf16[16,56,640]{2,1,0:T(8,128)(2,1)S(1)}, u32[]{:S(2)}, u32[]{:S(2)}) async-start(bf16[16,56,640]{2,1,0:T(8,128)(2,1)} %shard_map.96), calls=%async_computation.1 | async-start | bytes 2293760 | tf_op jit(solution)/shard_map/all_to_all | solution.py:140
  99.2 25.0 %copy-start.3 = (bf16[48,1024]{1,0:T(8,128)(2,1)S(1)}, bf16[48,1024]{1,0:T(8,128)(2,1)}, u32[]{:S(2)}) copy-start(bf16[48,1024]{1,0:T(8,128)(2,1)} %stream_ref.1) | copy-start | bytes 294916
  115.6 33.8 %collective-permute-start.13 = (bf16[4,8,16,512]{3,2,1,0:T(8,128)(2,1)S(1)}, bf16[4,8,16,512]{3,2,1,0:T(8,128)(2,1)}, u32[]{:S(2)}, u32[]{:S(2)}) collective-permute-start(bf16[4,8,16,512]{3,2,1,0:T(8,128)(2,1)S(1)} %slice.33), channel_id=1, source_target_pairs={{0,128},{128,256},{256,384},{384,0},{1,129},{129,257},{257,385},{3... | collective-permute-start | bytes 1572872 | tf_op jit(solution)/shard_map/ppermute | solution.py:206
  119.3 30.2 %collective-permute-start.14 = (bf16[4,8,16,512]{3,2,1,0:T(8,128)(2,1)S(1)}, bf16[4,8,16,512]{3,2,1,0:T(8,128)(2,1)S(1)}, u32[]{:S(2)}, u32[]{:S(2)}) collective-permute-start(bf16[4,8,16,512]{3,2,1,0:T(8,128)(2,1)S(1)} %slice.34), channel_id=1, source_target_pairs={{0,384},{128,0},{256,128},{384,256},{1,385},{129,1},{257,129},{385... | collective-permute-start | bytes 1572872 | tf_op jit(solution)/shard_map/ppermute | solution.py:206
  124.9 1.0 copy-start
  149.4 0.8 copy-start.9
  150.2 7.9 %copy-start.8 = (s32[1,48]{1,0:T(1,128)S(1)}, s32[1,48]{1,0:T(1,128)}, u32[]{:S(2)}) copy-start(s32[1,48]{1,0:T(1,128)} %starts_ref.1) | copy-start | bytes 580
  150.2 25.2 %copy-start.5 = (bf16[192,320]{1,0:T(8,128)(2,1)S(1)}, bf16[192,320]{1,0:T(8,128)(2,1)}, u32[]{:S(2)}) copy-start(bf16[192,320]{1,0:T(8,128)(2,1)} %param.14) | copy-start | bytes 368644
  156.0 3.4 %collective-permute-start.15 = (bf16[2,56,320]{2,1,0:T(8,128)(2,1)}, bf16[2,56,320]{2,1,0:T(8,128)(2,1)S(1)}, u32[]{:S(2)}, u32[]{:S(2)}) collective-permute-start(bf16[2,56,320]{2,1,0:T(8,128)(2,1)} %get-tuple-element.13), channel_id=1, source_target_pairs={{0,1},{1,0},{2,3},{3,2},{4,5},{5,4},{6,7},{7,6},{8,9},{9,8},{10,11... | collective-permute-start | bytes 215048 | tf_op jit(solution)/shard_map/ppermute | solution.py:225
  159.4 0.6 copy-start.6
  161.7 13.7 %collective-permute-start.16 = (bf16[56,320]{1,0:T(8,128)(2,1)}, bf16[56,320]{1,0:T(8,128)(2,1)S(1)}, u32[]{:S(2)}, u32[]{:S(2)}) collective-permute-start(bf16[56,320]{1,0:T(8,128)(2,1)} %get-tuple-element.15), channel_id=1, source_target_pairs={{0,2},{2,0},{1,3},{3,1},{4,6},{6,4},{5,7},{7,5},{8,10},{10,8},{9,1... | collective-permute-start | bytes 107528 | tf_op jit(solution)/shard_map/ppermute | solution.py:225

commit v3 on v2

--- a/solution.py
+++ b/solution.py
@@ -144,7 +144,7 @@
     return (distance & 1) * 4 + (distance & 2) + lax.div(distance, 4)
 
 
-def project_kernel(place_ref, attn_ref, own_ref, less_ref, more_ref, low_ref, high_ref, stream_ref, down_ref, out_ref, keep_ref, send_ref, new_ref):
+def project_kernel(place_ref, attn_ref, u0_ref, l0_ref, u1_ref, l1_ref, u2_ref, l2_ref, u3_ref, l3_ref, stream_ref, down_ref, out_ref, keep_ref, send_ref, new_ref):
     y, x, c, z = place_ref[0], place_ref[1], place_ref[2], place_ref[3]
     nt = (((1,), (1,)), ((), ()))
     span = 256
@@ -154,7 +154,7 @@
         total = stream_ref[:, at * span : (at + 1) * span].astype(jnp.float32)
         spots = [(turn, held_at((at * 2 + i) ^ z)) for i in range(2) for turn in turns]
         mixed = jnp.zeros_like(total)
-        for attn, refs in zip(heads, ((own_ref,), (more_ref,), (low_ref, high_ref), (less_ref,))):
+        for attn, refs in zip(heads, ((u0_ref, l0_ref), (u1_ref, l1_ref), (u2_ref, l2_ref), (u3_ref, l3_ref))):
             weight = jnp.concatenate([ref[turn, spot] for turn, spot in spots for ref in refs], axis=0)
             mixed = mixed + lax.dot_general(attn, weight, nt, preferred_element_type=jnp.float32)
         new_ref[:, at * span : (at + 1) * span] = (total + mixed).astype(jnp.bfloat16)
@@ -176,7 +176,7 @@
             jax.ShapeDtypeStruct((2, rows, 320), jnp.float32),
             jax.ShapeDtypeStruct((2, rows, 320), jnp.bfloat16),
         ),
-        in_specs=[SM] + [VM] * 8,
+        in_specs=[SM] + [VM] * 11,
         out_specs=(VM, VM, VM),
         scratch_shapes=[pltpu.VMEM((rows, width), jnp.bfloat16)],
         cost_estimate=pl.CostEstimate(flops=4_000_000_000, bytes_accessed=7_000_000, transcendentals=0),
@@ -216,9 +216,13 @@
 
 
 def plane_gathered(blocks):
-    own = jnp.stack([blocks] + [turned(blocks, "x", k) for k in (1, 2, 3)])
-    less, more = turned(own, "y", 1), turned(own, "y", -1)
-    return own, less, more, turned(less[:, :, :16], "y", 1), turned(more[:, :, 16:], "y", -1)
+    held = [blocks] + [turned(blocks, "x", k) for k in (1, 2, 3)]
+    upper = jnp.stack([block[:, :16] for block in held])
+    lower = jnp.stack([block[:, 16:] for block in held])
+    less_upper, more_lower = turned(upper, "y", 1), turned(lower, "y", -1)
+    less_lower, more_upper = turned(lower, "y", 1), turned(upper, "y", -1)
+    far_upper, far_lower = turned(less_upper, "y", 1), turned(more_lower, "y", -1)
+    return upper, lower, more_upper, more_lower, far_upper, far_lower, less_upper, less_lower
 
 
 def across(value, axis):

time: 178 us -> 187 us (1.051)
  the two profiles are of different devices: /device:TPU:1 before, /device:TPU:7 now
where the time goes in v3:
time: 187 us; the launch traced here: 186 us
  starting transfers between devices  93 us (50%)
  waiting for transfers between devices  43.1 us (23%)
  Pallas kernels  19.8 us (11%)
  blocking collectives  18.4 us (10%)
  local copies, waits for them, and re-layouts  4.8 us (3%)
  other arithmetic  3.78 us (2%)
    ppermute x9, starting transfers between devices, turned(): return lax.ppermute(value, axis, [(i, (i + by) % 4) for i in range(4)])  27.2 us
    ppermute x6, starting transfers between devices, line_halves(): other = lax.ppermute(held, 'z', [(i, i ^ bit) for i in range(8)])  26.8 us
    all_to_all x2, starting transfers between devices, exchange(): return lax.all_to_all(value, axes, split_axis=0, concat_axis=0, tiled=True)  24.1 us
    all_gather x1, blocking collectives, on_device(): attn = lax.all_gather(attn, TP, axis=0)  18.4 us
    ppermute x9, waiting for transfers between devices, turned(): return lax.ppermute(value, axis, [(i, (i + by) % 4) for i in range(4)])  17.6 us
    ppermute x6, waiting for transfers between devices, line_halves(): other = lax.ppermute(held, 'z', [(i, i ^ bit) for i in range(8)])  13.2 us
    ppermute x2, waiting for transfers between devices, across(): return lax.ppermute(value, axis, [(0, 1), (1, 0)])  11.6 us
    pallas_call x1, Pallas kernels, attend(): pl.pallas_call(attend_kernel, out_shape=jax.ShapeDtypeStruct((blocks, row...  7.92 us
  transfers between devices with their start and end apart: 21, of which 10 were waited for; matrix products, arithmetic and copies ran while one was open for 3% of the time, Pallas kernels for 1%

profile of v3, /device:TPU:7, one launch (start us, length us, event | category | flops | bytes accessed | tf_op | source)
XLA Modules:
  0.0 185.6 jit_solution(2302074034702568413)
XLA Ops:
  0.6 1.8 shard_map.95
  2.4 3.4 %collective-permute-start = (bf16[1,1536]{1,0:T(2,128)(2,1)}, bf16[1,1536]{1,0:T(2,128)(2,1)S(1)}, u32[]{:S(2)}, u32[]{:S(2)}) collective-permute-start(bf16[1,1536]{1,0:T(2,128)(2,1)} %get-tuple-element.9), channel_id=1, source_target_pairs={{0,4},{4,8},{8,12},{12,16},{16,20},{20,24},{24,28},{28,32},{32,36}... | collective-permute-start | bytes 9224 | tf_op jit(solution)/shard_map/ppermute | solution.py:240
  5.9 8.8 %collective-permute-start.1 = (bf16[1,48,1024]{2,1,0:T(8,128)(2,1)}, bf16[1,48,1024]{2,1,0:T(8,128)(2,1)S(1)}, u32[]{:S(2)}, u32[]{:S(2)}) collective-permute-start(bf16[1,48,1024]{2,1,0:T(8,128)(2,1)} %get-tuple-element.10), channel_id=1, source_target_pairs={{0,64},{16,80},{32,96},{48,112},{64,0},{80,16},{96,32},{112,48},{1... | collective-permute-start | bytes 294920 | tf_op jit(solution)/shard_map/ppermute | solution.py:212
  14.7 4.3 %collective-permute-start.4 = (bf16[32,512]{1,0:T(8,128)(2,1)}, bf16[32,512]{1,0:T(8,128)(2,1)S(1)}, u32[]{:S(2)}, u32[]{:S(2)}) collective-permute-start(bf16[32,512]{1,0:T(8,128)(2,1)} %bitcast.38), channel_id=1, source_target_pairs={{0,0},{1,128},{2,256},{3,384},{128,1},{129,129},{130,257},{131,385... | collective-permute-start | bytes 98312 | tf_op jit(solution)/shard_map/ppermute | solution.py:236
  19.1 0.9 constant_dynamic-update-slice_fusion.2
  20.0 0.6 fusion.5.key_ids_ref
  20.6 0.6 collective-permute-done.4
  21.1 1.9 %collective-permute-start.5 = (bf16[1,32,512]{2,1,0:T(8,128)(2,1)S(1)}, bf16[1,32,512]{2,1,0:T(8,128)(2,1)S(1)}, u32[]{:S(2)}, u32[]{:S(2)}) collective-permute-start(bf16[1,32,512]{2,1,0:T(8,128)(2,1)S(1)} %bitcast.31), channel_id=1, source_target_pairs={{0,64},{16,80},{32,96},{48,112},{64,0},{80,16},{96,32},{112,48},{1... | collective-permute-start | bytes 98312 | tf_op jit(solution)/shard_map/ppermute | solution.py:212
  23.1 0.6 pad_add_fusion.3.place_ref
  23.6 0.1 pad.31.clone
  23.7 0.0 collective-permute-done
  23.7 6.0 %collective-permute-done.5 = bf16[1,32,512]{2,1,0:T(8,128)(2,1)S(1)} collective-permute-done((bf16[1,32,512]{2,1,0:T(8,128)(2,1)S(1)}, bf16[1,32,512]{2,1,0:T(8,128)(2,1)S(1)}, u32[]{:S(2)}, u32[]{:S(2)}) %collective-permute-start.5) | collective-permute-done | bytes 32800 | tf_op jit(solution)/shard_map/ppermute | solution.py:212
  29.7 4.6 %collective-permute-start.6 = (bf16[2,32,512]{2,1,0:T(8,128)(2,1)S(1)}, bf16[2,32,512]{2,1,0:T(8,128)(2,1)S(1)}, u32[]{:S(2)}, u32[]{:S(2)}) collective-permute-start(bf16[2,32,512]{2,1,0:T(8,128)(2,1)S(1)} %pad_maximum_fusion.5), channel_id=1, source_target_pairs={{0,32},{16,48},{32,0},{48,16},{64,96},{80,112},{96,64},{112,80},{1... | collective-permute-start | bytes 196616 | tf_op jit(solution)/shard_map/ppermute | solution.py:212
  34.3 0.9 maximum_maximum_fusion.1
  35.2 1.0 broadcast_in_dim.11
  36.2 16.6 %all-to-all-start = ((bf16[16,56,512]{2,1,0:T(8,128)(2,1)}), bf16[16,56,512]{2,1,0:T(8,128)(2,1)S(1)}, u32[]{:S(2)}, u32[]{:S(2)}) async-start(bf16[16,56,512]{2,1,0:T(8,128)(2,1)} %broadcast_in_dim.11), calls=%async_computation | async-start | bytes 1835008 | tf_op jit(solution)/shard_map/all_to_all | solution.py:140
  52.8 0.0 collective-permute-done.6
  52.8 7.6 %collective-permute-start.7 = (bf16[4,32,512]{2,1,0:T(8,128)(2,1)S(1)}, bf16[4,32,512]{2,1,0:T(8,128)(2,1)S(1)}, u32[]{:S(2)}, u32[]{:S(2)}) collective-permute-start(bf16[4,32,512]{2,1,0:T(8,128)(2,1)S(1)} %pad_maximum_fusion.4), channel_id=1, source_target_pairs={{0,16},{16,0},{32,48},{48,32},{64,80},{80,64},{96,112},{112,96},{1... | collective-permute-start | bytes 393224 | tf_op jit(solution)/shard_map/ppermute | solution.py:212
  60.4 0.0 collective-permute-done.1
  60.5 1.9 %collective-permute-start.2 = (bf16[2,48,1024]{2,1,0:T(8,128)(2,1)S(1)}, bf16[2,48,1024]{2,1,0:T(8,128)(2,1)S(1)}, u32[]{:S(2)}, u32[]{:S(2)}) collective-permute-start(bf16[2,48,1024]{2,1,0:T(8,128)(2,1)S(1)} %pad_maximum_fusion.3), channel_id=1, source_target_pairs={{0,32},{16,48},{32,0},{48,16},{64,96},{80,112},{96,64},{112,80},{1... | collective-permute-start | bytes 589832 | tf_op jit(solution)/shard_map/ppermute | solution.py:212
  62.4 0.6 collective-permute-done.7
  63.1 2.5 %collective-permute-start.10 = (bf16[8,32,512]{2,1,0:T(8,128)(2,1)S(1)}, bf16[8,32,512]{2,1,0:T(8,128)(2,1)S(1)}, u32[]{:S(2)}, u32[]{:S(2)}) collective-permute-start(bf16[8,32,512]{2,1,0:T(8,128)(2,1)S(1)} %pad_maximum_fusion.2), channel_id=1, source_target_pairs={{0,12},{4,0},{8,4},{12,8},{1,13},{5,1},{9,5},{13,9},{2,14},{6,2},{... | collective-permute-start | bytes 786440 | tf_op jit(solution)/shard_map/ppermute | solution.py:206
  65.6 2.7 %collective-permute-start.9 = (bf16[8,32,512]{2,1,0:T(8,128)(2,1)S(1)}, bf16[8,32,512]{2,1,0:T(8,128)(2,1)S(1)}, u32[]{:S(2)}, u32[]{:S(2)}) collective-permute-start(bf16[8,32,512]{2,1,0:T(8,128)(2,1)S(1)} %pad_maximum_fusion.2), channel_id=1, source_target_pairs={{0,8},{4,12},{8,0},{12,4},{1,9},{5,13},{9,1},{13,5},{2,10},{6,14},... | collective-permute-start | bytes 786440 | tf_op jit(solution)/shard_map/ppermute | solution.py:206
  68.4 3.7 %collective-permute-start.8 = (bf16[8,32,512]{2,1,0:T(8,128)(2,1)S(1)}, bf16[8,32,512]{2,1,0:T(8,128)(2,1)S(1)}, u32[]{:S(2)}, u32[]{:S(2)}) collective-permute-start(bf16[8,32,512]{2,1,0:T(8,128)(2,1)S(1)} %pad_maximum_fusion.2), channel_id=1, source_target_pairs={{0,4},{4,8},{8,12},{12,0},{1,5},{5,9},{9,13},{13,1},{2,6},{6,10},{... | collective-permute-start | bytes 786440 | tf_op jit(solution)/shard_map/ppermute | solution.py:206
  72.1 1.5 collective-permute-done.2
  73.7 1.9 %collective-permute-start.3 = (bf16[4,48,1024]{2,1,0:T(8,128)(2,1)S(1)}, bf16[4,48,1024]{2,1,0:T(8,128)(2,1)}, u32[]{:S(2)}, u32[]{:S(2)}) collective-permute-start(bf16[4,48,1024]{2,1,0:T(8,128)(2,1)S(1)} %constant_dynamic-update-slice_fusion.near_ref), channel_id=1, source_target_pairs={{0,16},{16,0},{32,48},{48,32},{64,80},{80,64},{96,112},{112,96},{1... | collective-permute-start | bytes 1179656 | tf_op jit(solution)/shard_map/ppermute | solution.py:212
  75.6 0.0 collective-permute-done.10
  75.7 1.7 collective-permute-done.9
  77.4 1.2 collective-permute-done.8
  78.6 5.1 %collective-permute-done.3.far_ref = bf16[4,48,1024]{2,1,0:T(8,128)(2,1)} collective-permute-done((bf16[4,48,1024]{2,1,0:T(8,128)(2,1)S(1)}, bf16[4,48,1024]{2,1,0:T(8,128)(2,1)}, u32[]{:S(2)}, u32[]{:S(2)}) %collective-permute-start.3) | collective-permute-done | bytes 393248 | tf_op jit(solution)/shard_map/ppermute | solution.py:212
  83.7 0.0 all-to-all-done.q_ref
  83.7 0.9 copy-done.1
  84.6 7.9 %shard_map.96 = bf16[16,56,640]{2,1,0:T(8,128)(2,1)} custom-call(s32[2]{0:T(128)} %pad_add_fusion.3.place_ref, s32[1,384]{1,0:T(1,128)} %fusion.5.key_ids_ref, bf16[16,56,512]{2,1,0:T(8,128)(2,1)} %copy-done.1, bf16[4,48,1024]{2,1,0:T(8,128)(2,1)} %copy-done.8, bf16[4,48,1024]{2,1,0:T(8,128)(2,1)} %collective-permute-done.3.far_ref), custom_call_target="tpu_custom_call" | custom-call | flops 4000000000 | bytes 3000000 | tf_op jit(solution)/shard_map/pallas_call | solution.py:119
  92.6 7.5 %all-to-all-start.1 = ((bf16[16,56,640]{2,1,0:T(8,128)(2,1)}), bf16[16,56,640]{2,1,0:T(8,128)(2,1)S(1)}, u32[]{:S(2)}, u32[]{:S(2)}) async-start(bf16[16,56,640]{2,1,0:T(8,128)(2,1)} %shard_map.96), calls=%async_computation.1 | async-start | bytes 2293760 | tf_op jit(solution)/shard_map/all_to_all | solution.py:140
  100.1 0.1 pad_maximum_fusion.u0_ref
  100.2 3.1 %collective-permute-start.13 = (bf16[4,8,16,512]{3,2,1,0:T(8,128)(2,1)S(1)}, bf16[4,8,16,512]{3,2,1,0:T(8,128)(2,1)}, u32[]{:S(2)}, u32[]{:S(2)}) collective-permute-start(bf16[4,8,16,512]{3,2,1,0:T(8,128)(2,1)S(1)} %pad_maximum_fusion.u0_ref), channel_id=1, source_target_pairs={{0,128},{128,256},{256,384},{384,0},{1,129},{129,257},{257,385},{3... | collective-permute-start | bytes 1572872 | tf_op jit(solution)/shard_map/ppermute | solution.py:206
  103.3 0.1 pad_maximum_fusion.1.l0_ref
  103.3 3.4 %collective-permute-start.12 = (bf16[4,8,16,512]{3,2,1,0:T(8,128)(2,1)S(1)}, bf16[4,8,16,512]{3,2,1,0:T(8,128)(2,1)S(1)}, u32[]{:S(2)}, u32[]{:S(2)}) collective-permute-start(bf16[4,8,16,512]{3,2,1,0:T(8,128)(2,1)S(1)} %pad_maximum_fusion.1.l0_ref), channel_id=1, source_target_pairs={{0,384},{128,0},{256,128},{384,256},{1,385},{129,1},{257,129},{385... | collective-permute-start | bytes 1572872 | tf_op jit(solution)/shard_map/ppermute | solution.py:206
  106.8 3.1 %collective-permute-start.11 = (bf16[4,8,16,512]{3,2,1,0:T(8,128)(2,1)S(1)}, bf16[4,8,16,512]{3,2,1,0:T(8,128)(2,1)}, u32[]{:S(2)}, u32[]{:S(2)}) collective-permute-start(bf16[4,8,16,512]{3,2,1,0:T(8,128)(2,1)S(1)} %pad_maximum_fusion.u0_ref), channel_id=1, source_target_pairs={{0,384},{128,0},{256,128},{384,256},{1,385},{129,1},{257,129},{385... | collective-permute-start | bytes 1572872 | tf_op jit(solution)/shard_map/ppermute | solution.py:206
  109.9 2.2 %collective-permute-start.16 = (bf16[4,8,16,512]{3,2,1,0:T(8,128)(2,1)S(1)}, bf16[4,8,16,512]{3,2,1,0:T(8,128)(2,1)}, u32[]{:S(2)}, u32[]{:S(2)}) collective-permute-start(bf16[4,8,16,512]{3,2,1,0:T(8,128)(2,1)S(1)} %pad_maximum_fusion.1.l0_ref), channel_id=1, source_target_pairs={{0,128},{128,256},{256,384},{384,0},{1,129},{129,257},{257,385},{3... | collective-permute-start | bytes 1572872 | tf_op jit(solution)/shard_map/ppermute | solution.py:206
  112.1 14.7 %collective-permute-done.13.u3_ref = bf16[4,8,16,512]{3,2,1,0:T(8,128)(2,1)} collective-permute-done((bf16[4,8,16,512]{3,2,1,0:T(8,128)(2,1)S(1)}, bf16[4,8,16,512]{3,2,1,0:T(8,128)(2,1)}, u32[]{:S(2)}, u32[]{:S(2)}) %collective-permute-start.13) | collective-permute-done | bytes 524320 | tf_op jit(solution)/shard_map/ppermute | solution.py:206
  126.8 1.9 %collective-permute-start.14 = (bf16[4,8,16,512]{3,2,1,0:T(8,128)(2,1)}, bf16[4,8,16,512]{3,2,1,0:T(8,128)(2,1)}, u32[]{:S(2)}, u32[]{:S(2)}) collective-permute-start(bf16[4,8,16,512]{3,2,1,0:T(8,128)(2,1)} %collective-permute-done.13.u3_ref), channel_id=1, source_target_pairs={{0,128},{128,256},{256,384},{384,0},{1,129},{129,257},{257,385},{3... | collective-permute-start | bytes 1572872 | tf_op jit(solution)/shard_map/ppermute | solution.py:206
  128.7 4.6 %collective-permute-start.15 = (bf16[4,8,16,512]{3,2,1,0:T(8,128)(2,1)S(1)}, bf16[4,8,16,512]{3,2,1,0:T(8,128)(2,1)}, u32[]{:S(2)}, u32[]{:S(2)}) collective-permute-start(bf16[4,8,16,512]{3,2,1,0:T(8,128)(2,1)S(1)} %collective-permute-done.12.l1_ref), channel_id=1, source_target_pairs={{0,384},{128,0},{256,128},{384,256},{1,385},{129,1},{257,129},{385... | collective-permute-start | bytes 1572872 | tf_op jit(solution)/shard_map/ppermute | solution.py:206
  133.3 0.7 pad_add_fusion.2.place_ref
  134.0 0.7 maximum_maximum_fusion.stream_ref
  134.7 1.0 copy-done
  135.7 2.6 %shard_map.97 = bf16[56,512]{1,0:T(8,128)(2,1)} custom-call(bf16[16,56,640]{2,1,0:T(8,128)(2,1)} %copy-done), custom_call_target="tpu_custom_call" | custom-call | flops 2000000000 | bytes 1200000 | tf_op jit(solution)/shard_map/pallas_call | solution.py:130
  138.4 18.4 %all-gather = bf16[224,512]{1,0:T(8,128)(2,1)} all-gather(bf16[56,512]{1,0:T(8,128)(2,1)} %shard_map.97), channel_id=2, replica_groups=mesh['y'=4,'z'=8,'x'=4,'h'=2,'c'=2] {'h','c'}, dimensions={0}, use_global_device_ids=true | all-gather | bytes 286720 | tf_op jit(solution)/shard_map/all_gather | solution.py:255
  156.8 0.0 collective-permute-done.11.u1_ref
  156.8 0.0 collective-permute-done.16.l3_ref
  156.8 0.0 collective-permute-done.14.u2_ref
  156.8 0.0 collective-permute-done.15.l2_ref
  156.8 0.0 copy-start.9
  156.8 0.0 copy-start.6
  156.8 5.8 %shard_map.98 = (bf16[48,1024]{1,0:T(8,128)(2,1)}, f32[2,56,320]{2,1,0:T(8,128)}, bf16[2,56,320]{2,1,0:T(8,128)(2,1)}) custom-call(s32[4]{0:T(128)} %pad_add_fusion.2.place_ref, bf16[4,56,512]{2,1,0:T(8,128)(2,1)} %bitcast.35, bf16[4,8,16,512]{3,2,1,0:T(8,128)(2,1)} %copy-done.2, bf16[4,8,16,512]{3,2,1,0:T(8,128)(2,1)} %copy-done.3, ...), custom_call_target="tpu_custom_call" | custom-call | flops 4000000000 | bytes 7000000 | tf_op jit(solution)/shard_map/pallas_call | solution.py:172
  162.6 2.1 %collective-permute-start.17 = (bf16[2,56,320]{2,1,0:T(8,128)(2,1)}, bf16[2,56,320]{2,1,0:T(8,128)(2,1)S(1)}, u32[]{:S(2)}, u32[]{:S(2)}) collective-permute-start(bf16[2,56,320]{2,1,0:T(8,128)(2,1)} %get-tuple-element.13), channel_id=1, source_target_pairs={{0,1},{1,0},{2,3},{3,2},{4,5},{5,4},{6,7},{7,6},{8,9},{9,8},{10,11... | collective-permute-start | bytes 215048 | tf_op jit(solution)/shard_map/ppermute | solution.py:229
  164.7 0.1 slice_bitcast_fusion.8
  164.8 1.2 collective-permute-done.17.arrived_ref
  166.0 0.6 copy-done.7
  166.7 1.6 shard_map.99
  168.3 5.1 %collective-permute-start.18 = (bf16[56,320]{1,0:T(8,128)(2,1)}, bf16[56,320]{1,0:T(8,128)(2,1)S(1)}, u32[]{:S(2)}, u32[]{:S(2)}) collective-permute-start(bf16[56,320]{1,0:T(8,128)(2,1)} %get-tuple-element.15), channel_id=1, source_target_pairs={{0,2},{2,0},{1,3},{3,1},{4,6},{6,4},{5,7},{7,5},{8,10},{10,8},{9,1... | collective-permute-start | bytes 107528 | tf_op jit(solution)/shard_map/ppermute | solution.py:229
  173.4 0.1 pad_add_fusion.1
  173.5 10.4 %collective-permute-done.18 = bf16[56,320]{1,0:T(8,128)(2,1)S(1)} collective-permute-done((bf16[56,320]{1,0:T(8,128)(2,1)}, bf16[56,320]{1,0:T(8,128)(2,1)S(1)}, u32[]{:S(2)}, u32[]{:S(2)}) %collective-permute-start.18) | collective-permute-done | bytes 35872 | tf_op jit(solution)/shard_map/ppermute | solution.py:229
  183.9 1.7 fusion
  (33 shorter events, 0.2 us)
Async XLA Ops:
  2.4 21.3 %collective-permute-start = (bf16[1,1536]{1,0:T(2,128)(2,1)}, bf16[1,1536]{1,0:T(2,128)(2,1)S(1)}, u32[]{:S(2)}, u32[]{:S(2)}) collective-permute-start(bf16[1,1536]{1,0:T(2,128)(2,1)} %get-tuple-element.9), channel_id=1, source_target_pairs={{0,4},{4,8},{8,12},{12,16},{16,20},{20,24},{24,28},{28,32},{32,36}... | collective-permute-start | bytes 9224 | tf_op jit(solution)/shard_map/ppermute | solution.py:240
  5.9 54.6 %collective-permute-start.1 = (bf16[1,48,1024]{2,1,0:T(8,128)(2,1)}, bf16[1,48,1024]{2,1,0:T(8,128)(2,1)S(1)}, u32[]{:S(2)}, u32[]{:S(2)}) collective-permute-start(bf16[1,48,1024]{2,1,0:T(8,128)(2,1)} %get-tuple-element.10), channel_id=1, source_target_pairs={{0,64},{16,80},{32,96},{48,112},{64,0},{80,16},{96,32},{112,48},{1... | collective-permute-start | bytes 294920 | tf_op jit(solution)/shard_map/ppermute | solution.py:212
  14.7 6.4 %collective-permute-start.4 = (bf16[32,512]{1,0:T(8,128)(2,1)}, bf16[32,512]{1,0:T(8,128)(2,1)S(1)}, u32[]{:S(2)}, u32[]{:S(2)}) collective-permute-start(bf16[32,512]{1,0:T(8,128)(2,1)} %bitcast.38), channel_id=1, source_target_pairs={{0,0},{1,128},{2,256},{3,384},{128,1},{129,129},{130,257},{131,385... | collective-permute-start | bytes 98312 | tf_op jit(solution)/shard_map/ppermute | solution.py:236
  21.1 8.6 %collective-permute-start.5 = (bf16[1,32,512]{2,1,0:T(8,128)(2,1)S(1)}, bf16[1,32,512]{2,1,0:T(8,128)(2,1)S(1)}, u32[]{:S(2)}, u32[]{:S(2)}) collective-permute-start(bf16[1,32,512]{2,1,0:T(8,128)(2,1)S(1)} %bitcast.31), channel_id=1, source_target_pairs={{0,64},{16,80},{32,96},{48,112},{64,0},{80,16},{96,32},{112,48},{1... | collective-permute-start | bytes 98312 | tf_op jit(solution)/shard_map/ppermute | solution.py:212
  29.7 23.1 %collective-permute-start.6 = (bf16[2,32,512]{2,1,0:T(8,128)(2,1)S(1)}, bf16[2,32,512]{2,1,0:T(8,128)(2,1)S(1)}, u32[]{:S(2)}, u32[]{:S(2)}) collective-permute-start(bf16[2,32,512]{2,1,0:T(8,128)(2,1)S(1)} %pad_maximum_fusion.5), channel_id=1, source_target_pairs={{0,32},{16,48},{32,0},{48,16},{64,96},{80,112},{96,64},{112,80},{1... | collective-permute-start | bytes 196616 | tf_op jit(solution)/shard_map/ppermute | solution.py:212
  36.2 24.3 %copy-start.5 = (bf16[1,48,1024]{2,1,0:T(8,128)(2,1)S(1)}, bf16[1,48,1024]{2,1,0:T(8,128)(2,1)}, u32[]{:S(2)}) copy-start(bf16[1,48,1024]{2,1,0:T(8,128)(2,1)} %get-tuple-element.10) | copy-start | bytes 294916
  36.2 47.5 %all-to-all-start = ((bf16[16,56,512]{2,1,0:T(8,128)(2,1)}), bf16[16,56,512]{2,1,0:T(8,128)(2,1)S(1)}, u32[]{:S(2)}, u32[]{:S(2)}) async-start(bf16[16,56,512]{2,1,0:T(8,128)(2,1)} %broadcast_in_dim.11), calls=%async_computation | async-start | bytes 1835008 | tf_op jit(solution)/shard_map/all_to_all | solution.py:140
  52.8 10.2 %collective-permute-start.7 = (bf16[4,32,512]{2,1,0:T(8,128)(2,1)S(1)}, bf16[4,32,512]{2,1,0:T(8,128)(2,1)S(1)}, u32[]{:S(2)}, u32[]{:S(2)}) collective-permute-start(bf16[4,32,512]{2,1,0:T(8,128)(2,1)S(1)} %pad_maximum_fusion.4), channel_id=1, source_target_pairs={{0,16},{16,0},{32,48},{48,32},{64,80},{80,64},{96,112},{112,96},{1... | collective-permute-start | bytes 393224 | tf_op jit(solution)/shard_map/ppermute | solution.py:212
  60.5 13.2 %collective-permute-start.2 = (bf16[2,48,1024]{2,1,0:T(8,128)(2,1)S(1)}, bf16[2,48,1024]{2,1,0:T(8,128)(2,1)S(1)}, u32[]{:S(2)}, u32[]{:S(2)}) collective-permute-start(bf16[2,48,1024]{2,1,0:T(8,128)(2,1)S(1)} %pad_maximum_fusion.3), channel_id=1, source_target_pairs={{0,32},{16,48},{32,0},{48,16},{64,96},{80,112},{96,64},{112,80},{1... | collective-permute-start | bytes 589832 | tf_op jit(solution)/shard_map/ppermute | solution.py:212
  63.1 12.5 %collective-permute-start.10 = (bf16[8,32,512]{2,1,0:T(8,128)(2,1)S(1)}, bf16[8,32,512]{2,1,0:T(8,128)(2,1)S(1)}, u32[]{:S(2)}, u32[]{:S(2)}) collective-permute-start(bf16[8,32,512]{2,1,0:T(8,128)(2,1)S(1)} %pad_maximum_fusion.2), channel_id=1, source_target_pairs={{0,12},{4,0},{8,4},{12,8},{1,13},{5,1},{9,5},{13,9},{2,14},{6,2},{... | collective-permute-start | bytes 786440 | tf_op jit(solution)/shard_map/ppermute | solution.py:206
  65.6 11.8 %collective-permute-start.9 = (bf16[8,32,512]{2,1,0:T(8,128)(2,1)S(1)}, bf16[8,32,512]{2,1,0:T(8,128)(2,1)S(1)}, u32[]{:S(2)}, u32[]{:S(2)}) collective-permute-start(bf16[8,32,512]{2,1,0:T(8,128)(2,1)S(1)} %pad_maximum_fusion.2), channel_id=1, source_target_pairs={{0,8},{4,12},{8,0},{12,4},{1,9},{5,13},{9,1},{13,5},{2,10},{6,14},... | collective-permute-start | bytes 786440 | tf_op jit(solution)/shard_map/ppermute | solution.py:206
  68.4 10.2 %collective-permute-start.8 = (bf16[8,32,512]{2,1,0:T(8,128)(2,1)S(1)}, bf16[8,32,512]{2,1,0:T(8,128)(2,1)S(1)}, u32[]{:S(2)}, u32[]{:S(2)}) collective-permute-start(bf16[8,32,512]{2,1,0:T(8,128)(2,1)S(1)} %pad_maximum_fusion.2), channel_id=1, source_target_pairs={{0,4},{4,8},{8,12},{12,0},{1,5},{5,9},{9,13},{13,1},{2,6},{6,10},{... | collective-permute-start | bytes 786440 | tf_op jit(solution)/shard_map/ppermute | solution.py:206
  73.7 10.0 %copy-start.8 = (bf16[4,48,1024]{2,1,0:T(8,128)(2,1)}, bf16[4,48,1024]{2,1,0:T(8,128)(2,1)S(1)}, u32[]{:S(2)}) copy-start(bf16[4,48,1024]{2,1,0:T(8,128)(2,1)S(1)} %constant_dynamic-update-slice_fusion.near_ref) | copy-start | bytes 1179652
  73.7 10.0 %collective-permute-start.3 = (bf16[4,48,1024]{2,1,0:T(8,128)(2,1)S(1)}, bf16[4,48,1024]{2,1,0:T(8,128)(2,1)}, u32[]{:S(2)}, u32[]{:S(2)}) collective-permute-start(bf16[4,48,1024]{2,1,0:T(8,128)(2,1)S(1)} %constant_dynamic-update-slice_fusion.near_ref), channel_id=1, source_target_pairs={{0,16},{16,0},{32,48},{48,32},{64,80},{80,64},{96,112},{112,96},{1... | collective-permute-start | bytes 1179656 | tf_op jit(solution)/shard_map/ppermute | solution.py:212
  83.7 0.9 copy-start.1
  92.6 42.1 %all-to-all-start.1 = ((bf16[16,56,640]{2,1,0:T(8,128)(2,1)}), bf16[16,56,640]{2,1,0:T(8,128)(2,1)S(1)}, u32[]{:S(2)}, u32[]{:S(2)}) async-start(bf16[16,56,640]{2,1,0:T(8,128)(2,1)} %shard_map.96), calls=%async_computation.1 | async-start | bytes 2293760 | tf_op jit(solution)/shard_map/all_to_all | solution.py:140
  100.1 33.9 %copy-start.4 = (bf16[48,1024]{1,0:T(8,128)(2,1)S(1)}, bf16[48,1024]{1,0:T(8,128)(2,1)}, u32[]{:S(2)}) copy-start(bf16[48,1024]{1,0:T(8,128)(2,1)} %stream_ref.1) | copy-start | bytes 294916
  100.2 38.2 %copy-start.2 = (bf16[4,8,16,512]{3,2,1,0:T(8,128)(2,1)}, bf16[4,8,16,512]{3,2,1,0:T(8,128)(2,1)S(1)}, u32[]{:S(2)}) copy-start(bf16[4,8,16,512]{3,2,1,0:T(8,128)(2,1)S(1)} %pad_maximum_fusion.u0_ref) | copy-start | bytes 1572868
  100.2 26.6 %collective-permute-start.13 = (bf16[4,8,16,512]{3,2,1,0:T(8,128)(2,1)S(1)}, bf16[4,8,16,512]{3,2,1,0:T(8,128)(2,1)}, u32[]{:S(2)}, u32[]{:S(2)}) collective-permute-start(bf16[4,8,16,512]{3,2,1,0:T(8,128)(2,1)S(1)} %pad_maximum_fusion.u0_ref), channel_id=1, source_target_pairs={{0,128},{128,256},{256,384},{384,0},{1,129},{129,257},{257,385},{3... | collective-permute-start | bytes 1572872 | tf_op jit(solution)/shard_map/ppermute | solution.py:206
  103.3 35.0 %copy-start.3 = (bf16[4,8,16,512]{3,2,1,0:T(8,128)(2,1)}, bf16[4,8,16,512]{3,2,1,0:T(8,128)(2,1)S(1)}, u32[]{:S(2)}) copy-start(bf16[4,8,16,512]{3,2,1,0:T(8,128)(2,1)S(1)} %pad_maximum_fusion.1.l0_ref) | copy-start | bytes 1572868
  103.3 25.3 %collective-permute-start.12 = (bf16[4,8,16,512]{3,2,1,0:T(8,128)(2,1)S(1)}, bf16[4,8,16,512]{3,2,1,0:T(8,128)(2,1)S(1)}, u32[]{:S(2)}, u32[]{:S(2)}) collective-permute-start(bf16[4,8,16,512]{3,2,1,0:T(8,128)(2,1)S(1)} %pad_maximum_fusion.1.l0_ref), channel_id=1, source_target_pairs={{0,384},{128,0},{256,128},{384,256},{1,385},{129,1},{257,129},{385... | collective-permute-start | bytes 1572872 | tf_op jit(solution)/shard_map/ppermute | solution.py:206
  106.8 50.0 %collective-permute-start.11 = (bf16[4,8,16,512]{3,2,1,0:T(8,128)(2,1)S(1)}, bf16[4,8,16,512]{3,2,1,0:T(8,128)(2,1)}, u32[]{:S(2)}, u32[]{:S(2)}) collective-permute-start(bf16[4,8,16,512]{3,2,1,0:T(8,128)(2,1)S(1)} %pad_maximum_fusion.u0_ref), channel_id=1, source_target_pairs={{0,384},{128,0},{256,128},{384,256},{1,385},{129,1},{257,129},{385... | collective-permute-start | bytes 1572872 | tf_op jit(solution)/shard_map/ppermute | solution.py:206
  109.9 46.9 %collective-permute-start.16 = (bf16[4,8,16,512]{3,2,1,0:T(8,128)(2,1)S(1)}, bf16[4,8,16,512]{3,2,1,0:T(8,128)(2,1)}, u32[]{:S(2)}, u32[]{:S(2)}) collective-permute-start(bf16[4,8,16,512]{3,2,1,0:T(8,128)(2,1)S(1)} %pad_maximum_fusion.1.l0_ref), channel_id=1, source_target_pairs={{0,128},{128,256},{256,384},{384,0},{1,129},{129,257},{257,385},{3... | collective-permute-start | bytes 1572872 | tf_op jit(solution)/shard_map/ppermute | solution.py:206
  126.8 30.0 %collective-permute-start.14 = (bf16[4,8,16,512]{3,2,1,0:T(8,128)(2,1)}, bf16[4,8,16,512]{3,2,1,0:T(8,128)(2,1)}, u32[]{:S(2)}, u32[]{:S(2)}) collective-permute-start(bf16[4,8,16,512]{3,2,1,0:T(8,128)(2,1)} %collective-permute-done.13.u3_ref), channel_id=1, source_target_pairs={{0,128},{128,256},{256,384},{384,0},{1,129},{129,257},{257,385},{3... | collective-permute-start | bytes 1572872 | tf_op jit(solution)/shard_map/ppermute | solution.py:206
  128.7 9.7 %copy-start.10 = (bf16[4,8,16,512]{3,2,1,0:T(8,128)(2,1)}, bf16[4,8,16,512]{3,2,1,0:T(8,128)(2,1)S(1)}, u32[]{:S(2)}) copy-start(bf16[4,8,16,512]{3,2,1,0:T(8,128)(2,1)S(1)} %collective-permute-done.12.l1_ref) | copy-start | bytes 1572868
  128.7 28.1 %collective-permute-start.15 = (bf16[4,8,16,512]{3,2,1,0:T(8,128)(2,1)S(1)}, bf16[4,8,16,512]{3,2,1,0:T(8,128)(2,1)}, u32[]{:S(2)}, u32[]{:S(2)}) collective-permute-start(bf16[4,8,16,512]{3,2,1,0:T(8,128)(2,1)S(1)} %collective-permute-done.12.l1_ref), channel_id=1, source_target_pairs={{0,384},{128,0},{256,128},{384,256},{1,385},{129,1},{257,129},{385... | collective-permute-start | bytes 1572872 | tf_op jit(solution)/shard_map/ppermute | solution.py:206
  134.7 1.0 copy-start
  156.8 7.9 %copy-start.9 = (s32[1,48]{1,0:T(1,128)S(1)}, s32[1,48]{1,0:T(1,128)}, u32[]{:S(2)}) copy-start(s32[1,48]{1,0:T(1,128)} %starts_ref.1) | copy-start | bytes 580
  156.8 27.1 %copy-start.6 = (bf16[192,320]{1,0:T(8,128)(2,1)S(1)}, bf16[192,320]{1,0:T(8,128)(2,1)}, u32[]{:S(2)}) copy-start(bf16[192,320]{1,0:T(8,128)(2,1)} %param.14) | copy-start | bytes 368644
  162.6 3.4 %collective-permute-start.17 = (bf16[2,56,320]{2,1,0:T(8,128)(2,1)}, bf16[2,56,320]{2,1,0:T(8,128)(2,1)S(1)}, u32[]{:S(2)}, u32[]{:S(2)}) collective-permute-start(bf16[2,56,320]{2,1,0:T(8,128)(2,1)} %get-tuple-element.13), channel_id=1, source_target_pairs={{0,1},{1,0},{2,3},{3,2},{4,5},{5,4},{6,7},{7,6},{8,9},{9,8},{10,11... | collective-permute-start | bytes 215048 | tf_op jit(solution)/shard_map/ppermute | solution.py:229
  166.0 0.6 copy-start.7
  168.3 15.6 %collective-permute-start.18 = (bf16[56,320]{1,0:T(8,128)(2,1)}, bf16[56,320]{1,0:T(8,128)(2,1)S(1)}, u32[]{:S(2)}, u32[]{:S(2)}) collective-permute-start(bf16[56,320]{1,0:T(8,128)(2,1)} %get-tuple-element.15), channel_id=1, source_target_pairs={{0,2},{2,0},{1,3},{3,1},{4,6},{6,4},{5,7},{7,5},{8,10},{10,8},{9,1... | collective-permute-start | bytes 107528 | tf_op jit(solution)/shard_map/ppermute | solution.py:229

commit v4 on v3

--- a/solution.py
+++ b/solution.py
@@ -15,6 +15,7 @@
 ROWS = 48
 PAD = 56
 NEG = -1e30
+LOG2E = 1.4426950408889634
 FLOOR = -1e29
 MARK = 64.0
 LIMIT = 4096.0
@@ -60,10 +61,10 @@
             q = q_ref[at_blocks, :, h * DH : (h + 1) * DH].reshape(group * rows, DH)
             k = kv[:, h * DH : (h + 1) * DH]
             v = kv[:, width + h * DH : width + (h + 1) * DH]
-            s = lax.dot_general(q, k, nt, preferred_element_type=jnp.float32) * (DH**-0.5)
+            s = lax.dot_general(q, k, nt, preferred_element_type=jnp.float32) * (DH**-0.5 * LOG2E)
             s = jnp.where(allowed, s, NEG)
             peak = jnp.maximum(jnp.max(s, axis=1, keepdims=True), FLOOR).astype(jnp.bfloat16).astype(jnp.float32)
-            e = jnp.exp(s - peak)
+            e = jnp.exp2(s - peak)
             total = jnp.sum(e, axis=1, keepdims=True)
             o = jnp.dot(e.astype(jnp.bfloat16), v, preferred_element_type=jnp.float32)
             out_ref[at_blocks, :, h * DH : (h + 1) * DH] = o.astype(jnp.bfloat16).reshape(group, rows, DH)
@@ -83,7 +84,7 @@
     top = stats[0]
     for b in range(1, blocks):
         top = jnp.maximum(top, stats[b])
-    shares = [jnp.exp(jnp.minimum(stat - top, 0.0)) for stat in stats]
+    shares = [jnp.exp2(jnp.minimum(stat - top, 0.0)) for stat in stats]
     total = jnp.zeros_like(top)
     for share, stat in zip(shares, stats):
         total = total + share * (pltpu.roll(stat, DH - 1, 1) + pltpu.roll(stat, DH - 2, 1))

time: 187 us -> 186 us (level)
  the two profiles are of different devices: /device:TPU:7 before, /device:TPU:4 now
where the time goes in v4:
time: 186 us; the launch traced here: 185 us
  starting transfers between devices  99.6 us (54%)
  waiting for transfers between devices  38.9 us (21%)
  Pallas kernels  19.7 us (11%)
  blocking collectives  15.7 us (8%)
  local copies, waits for them, and re-layouts  4.8 us (3%)
  other arithmetic  3.78 us (2%)
    all_to_all x2, starting transfers between devices, exchange(): return lax.all_to_all(value, axes, split_axis=0, concat_axis=0, tiled=True)  29.6 us
    ppermute x6, starting transfers between devices, line_halves(): other = lax.ppermute(held, 'z', [(i, i ^ bit) for i in range(8)])  28.9 us
    ppermute x9, starting transfers between devices, turned(): return lax.ppermute(value, axis, [(i, (i + by) % 4) for i in range(4)])  28.9 us
    ppermute x9, waiting for transfers between devices, turned(): return lax.ppermute(value, axis, [(i, (i + by) % 4) for i in range(4)])  16.3 us
    all_gather x1, blocking collectives, on_device(): attn = lax.all_gather(attn, TP, axis=0)  15.7 us
    ppermute x6, waiting for transfers between devices, line_halves(): other = lax.ppermute(held, 'z', [(i, i ^ bit) for i in range(8)])  11.3 us
    ppermute x2, waiting for transfers between devices, across(): return lax.ppermute(value, axis, [(0, 1), (1, 0)])  11.3 us
    pallas_call x1, Pallas kernels, attend(): pl.pallas_call(attend_kernel, out_shape=jax.ShapeDtypeStruct((blocks, row...  7.88 us
  transfers between devices with their start and end apart: 21, of which 7 were waited for; matrix products, arithmetic and copies ran while one was open for 3% of the time, Pallas kernels for 1%

profile of v4, /device:TPU:4, one launch (start us, length us, event | category | flops | bytes accessed | tf_op | source)
XLA Modules:
  0.0 185.2 jit_solution(8801296339130445665)
XLA Ops:
  0.6 1.8 shard_map.95
  2.4 3.1 %collective-permute-start = (bf16[1,1536]{1,0:T(2,128)(2,1)}, bf16[1,1536]{1,0:T(2,128)(2,1)S(1)}, u32[]{:S(2)}, u32[]{:S(2)}) collective-permute-start(bf16[1,1536]{1,0:T(2,128)(2,1)} %get-tuple-element.9), channel_id=1, source_target_pairs={{0,4},{4,8},{8,12},{12,16},{16,20},{20,24},{24,28},{28,32},{32,36}... | collective-permute-start | bytes 9224 | tf_op jit(solution)/shard_map/ppermute | solution.py:241
  5.5 9.1 %collective-permute-start.1 = (bf16[1,48,1024]{2,1,0:T(8,128)(2,1)}, bf16[1,48,1024]{2,1,0:T(8,128)(2,1)S(1)}, u32[]{:S(2)}, u32[]{:S(2)}) collective-permute-start(bf16[1,48,1024]{2,1,0:T(8,128)(2,1)} %get-tuple-element.10), channel_id=1, source_target_pairs={{0,64},{16,80},{32,96},{48,112},{64,0},{80,16},{96,32},{112,48},{1... | collective-permute-start | bytes 294920 | tf_op jit(solution)/shard_map/ppermute | solution.py:213
  14.6 1.4 collective-permute-start.4
  16.1 0.9 constant_dynamic-update-slice_fusion.2
  17.0 0.6 fusion.5.key_ids_ref
  17.6 0.0 collective-permute-done.4
  17.6 1.9 %collective-permute-start.5 = (bf16[1,32,512]{2,1,0:T(8,128)(2,1)S(1)}, bf16[1,32,512]{2,1,0:T(8,128)(2,1)S(1)}, u32[]{:S(2)}, u32[]{:S(2)}) collective-permute-start(bf16[1,32,512]{2,1,0:T(8,128)(2,1)S(1)} %bitcast.31), channel_id=1, source_target_pairs={{0,64},{16,80},{32,96},{48,112},{64,0},{80,16},{96,32},{112,48},{1... | collective-permute-start | bytes 98312 | tf_op jit(solution)/shard_map/ppermute | solution.py:213
  19.5 0.6 pad_add_fusion.3.place_ref
  20.1 0.1 pad.31.clone
  20.1 0.0 collective-permute-done
  20.1 7.1 %collective-permute-done.5 = bf16[1,32,512]{2,1,0:T(8,128)(2,1)S(1)} collective-permute-done((bf16[1,32,512]{2,1,0:T(8,128)(2,1)S(1)}, bf16[1,32,512]{2,1,0:T(8,128)(2,1)S(1)}, u32[]{:S(2)}, u32[]{:S(2)}) %collective-permute-start.5) | collective-permute-done | bytes 32800 | tf_op jit(solution)/shard_map/ppermute | solution.py:213
  27.3 5.2 %collective-permute-start.6 = (bf16[2,32,512]{2,1,0:T(8,128)(2,1)S(1)}, bf16[2,32,512]{2,1,0:T(8,128)(2,1)S(1)}, u32[]{:S(2)}, u32[]{:S(2)}) collective-permute-start(bf16[2,32,512]{2,1,0:T(8,128)(2,1)S(1)} %pad_maximum_fusion.5), channel_id=1, source_target_pairs={{0,32},{16,48},{32,0},{48,16},{64,96},{80,112},{96,64},{112,80},{1... | collective-permute-start | bytes 196616 | tf_op jit(solution)/shard_map/ppermute | solution.py:213
  32.5 0.9 maximum_maximum_fusion.1
  33.4 1.0 broadcast_in_dim.11
  34.4 22.3 %all-to-all-start = ((bf16[16,56,512]{2,1,0:T(8,128)(2,1)}), bf16[16,56,512]{2,1,0:T(8,128)(2,1)S(1)}, u32[]{:S(2)}, u32[]{:S(2)}) async-start(bf16[16,56,512]{2,1,0:T(8,128)(2,1)} %broadcast_in_dim.11), calls=%async_computation | async-start | bytes 1835008 | tf_op jit(solution)/shard_map/all_to_all | solution.py:141
  56.7 0.0 collective-permute-done.6
  56.7 4.7 %collective-permute-start.7 = (bf16[4,32,512]{2,1,0:T(8,128)(2,1)S(1)}, bf16[4,32,512]{2,1,0:T(8,128)(2,1)S(1)}, u32[]{:S(2)}, u32[]{:S(2)}) collective-permute-start(bf16[4,32,512]{2,1,0:T(8,128)(2,1)S(1)} %pad_maximum_fusion.4), channel_id=1, source_target_pairs={{0,16},{16,0},{32,48},{48,32},{64,80},{80,64},{96,112},{112,96},{1... | collective-permute-start | bytes 393224 | tf_op jit(solution)/shard_map/ppermute | solution.py:213
  61.4 0.0 collective-permute-done.1
  61.5 4.2 %collective-permute-start.2 = (bf16[2,48,1024]{2,1,0:T(8,128)(2,1)S(1)}, bf16[2,48,1024]{2,1,0:T(8,128)(2,1)S(1)}, u32[]{:S(2)}, u32[]{:S(2)}) collective-permute-start(bf16[2,48,1024]{2,1,0:T(8,128)(2,1)S(1)} %pad_maximum_fusion.3), channel_id=1, source_target_pairs={{0,32},{16,48},{32,0},{48,16},{64,96},{80,112},{96,64},{112,80},{1... | collective-permute-start | bytes 589832 | tf_op jit(solution)/shard_map/ppermute | solution.py:213
  65.8 0.0 collective-permute-done.7
  65.8 2.5 %collective-permute-start.10 = (bf16[8,32,512]{2,1,0:T(8,128)(2,1)S(1)}, bf16[8,32,512]{2,1,0:T(8,128)(2,1)S(1)}, u32[]{:S(2)}, u32[]{:S(2)}) collective-permute-start(bf16[8,32,512]{2,1,0:T(8,128)(2,1)S(1)} %pad_maximum_fusion.2), channel_id=1, source_target_pairs={{0,12},{4,0},{8,4},{12,8},{1,13},{5,1},{9,5},{13,9},{2,14},{6,2},{... | collective-permute-start | bytes 786440 | tf_op jit(solution)/shard_map/ppermute | solution.py:207
  68.3 4.6 %collective-permute-start.9 = (bf16[8,32,512]{2,1,0:T(8,128)(2,1)S(1)}, bf16[8,32,512]{2,1,0:T(8,128)(2,1)S(1)}, u32[]{:S(2)}, u32[]{:S(2)}) collective-permute-start(bf16[8,32,512]{2,1,0:T(8,128)(2,1)S(1)} %pad_maximum_fusion.2), channel_id=1, source_target_pairs={{0,8},{4,12},{8,0},{12,4},{1,9},{5,13},{9,1},{13,5},{2,10},{6,14},... | collective-permute-start | bytes 786440 | tf_op jit(solution)/shard_map/ppermute | solution.py:207
  72.9 1.9 %collective-permute-start.8 = (bf16[8,32,512]{2,1,0:T(8,128)(2,1)S(1)}, bf16[8,32,512]{2,1,0:T(8,128)(2,1)S(1)}, u32[]{:S(2)}, u32[]{:S(2)}) collective-permute-start(bf16[8,32,512]{2,1,0:T(8,128)(2,1)S(1)} %pad_maximum_fusion.2), channel_id=1, source_target_pairs={{0,4},{4,8},{8,12},{12,0},{1,5},{5,9},{9,13},{13,1},{2,6},{6,10},{... | collective-permute-start | bytes 786440 | tf_op jit(solution)/shard_map/ppermute | solution.py:207
  74.8 0.0 collective-permute-done.2
  74.9 3.8 %collective-permute-start.3 = (bf16[4,48,1024]{2,1,0:T(8,128)(2,1)S(1)}, bf16[4,48,1024]{2,1,0:T(8,128)(2,1)}, u32[]{:S(2)}, u32[]{:S(2)}) collective-permute-start(bf16[4,48,1024]{2,1,0:T(8,128)(2,1)S(1)} %constant_dynamic-update-slice_fusion.near_ref), channel_id=1, source_target_pairs={{0,16},{16,0},{32,48},{48,32},{64,80},{80,64},{96,112},{112,96},{1... | collective-permute-start | bytes 1179656 | tf_op jit(solution)/shard_map/ppermute | solution.py:213
  78.7 0.0 collective-permute-done.10
  78.7 1.0 collective-permute-done.9
  79.7 2.7 %collective-permute-done.8 = bf16[8,32,512]{2,1,0:T(8,128)(2,1)S(1)} collective-permute-done((bf16[8,32,512]{2,1,0:T(8,128)(2,1)S(1)}, bf16[8,32,512]{2,1,0:T(8,128)(2,1)S(1)}, u32[]{:S(2)}, u32[]{:S(2)}) %collective-permute-start.8) | collective-permute-done | bytes 262176 | tf_op jit(solution)/shard_map/ppermute | solution.py:207
  82.4 4.1 %collective-permute-done.3.far_ref = bf16[4,48,1024]{2,1,0:T(8,128)(2,1)} collective-permute-done((bf16[4,48,1024]{2,1,0:T(8,128)(2,1)S(1)}, bf16[4,48,1024]{2,1,0:T(8,128)(2,1)}, u32[]{:S(2)}, u32[]{:S(2)}) %collective-permute-start.3) | collective-permute-done | bytes 393248 | tf_op jit(solution)/shard_map/ppermute | solution.py:213
  86.6 0.0 all-to-all-done.q_ref
  86.6 0.9 copy-done.1
  87.5 7.9 %shard_map.96 = bf16[16,56,640]{2,1,0:T(8,128)(2,1)} custom-call(s32[2]{0:T(128)} %pad_add_fusion.3.place_ref, s32[1,384]{1,0:T(1,128)} %fusion.5.key_ids_ref, bf16[16,56,512]{2,1,0:T(8,128)(2,1)} %copy-done.1, bf16[4,48,1024]{2,1,0:T(8,128)(2,1)} %copy-done.8, bf16[4,48,1024]{2,1,0:T(8,128)(2,1)} %collective-permute-done.3.far_ref), custom_call_target="tpu_custom_call" | custom-call | flops 4000000000 | bytes 3000000 | tf_op jit(solution)/shard_map/pallas_call | solution.py:120
  95.4 7.2 %all-to-all-start.1 = ((bf16[16,56,640]{2,1,0:T(8,128)(2,1)}), bf16[16,56,640]{2,1,0:T(8,128)(2,1)S(1)}, u32[]{:S(2)}, u32[]{:S(2)}) async-start(bf16[16,56,640]{2,1,0:T(8,128)(2,1)} %shard_map.96), calls=%async_computation.1 | async-start | bytes 2293760 | tf_op jit(solution)/shard_map/all_to_all | solution.py:141
  102.6 0.1 pad_maximum_fusion.u0_ref
  102.7 3.4 %collective-permute-start.13 = (bf16[4,8,16,512]{3,2,1,0:T(8,128)(2,1)S(1)}, bf16[4,8,16,512]{3,2,1,0:T(8,128)(2,1)}, u32[]{:S(2)}, u32[]{:S(2)}) collective-permute-start(bf16[4,8,16,512]{3,2,1,0:T(8,128)(2,1)S(1)} %pad_maximum_fusion.u0_ref), channel_id=1, source_target_pairs={{0,128},{128,256},{256,384},{384,0},{1,129},{129,257},{257,385},{3... | collective-permute-start | bytes 1572872 | tf_op jit(solution)/shard_map/ppermute | solution.py:207
  106.1 0.1 pad_maximum_fusion.1.l0_ref
  106.2 3.7 %collective-permute-start.12 = (bf16[4,8,16,512]{3,2,1,0:T(8,128)(2,1)S(1)}, bf16[4,8,16,512]{3,2,1,0:T(8,128)(2,1)S(1)}, u32[]{:S(2)}, u32[]{:S(2)}) collective-permute-start(bf16[4,8,16,512]{3,2,1,0:T(8,128)(2,1)S(1)} %pad_maximum_fusion.1.l0_ref), channel_id=1, source_target_pairs={{0,384},{128,0},{256,128},{384,256},{1,385},{129,1},{257,129},{385... | collective-permute-start | bytes 1572872 | tf_op jit(solution)/shard_map/ppermute | solution.py:207
  109.9 3.4 %collective-permute-start.11 = (bf16[4,8,16,512]{3,2,1,0:T(8,128)(2,1)S(1)}, bf16[4,8,16,512]{3,2,1,0:T(8,128)(2,1)}, u32[]{:S(2)}, u32[]{:S(2)}) collective-permute-start(bf16[4,8,16,512]{3,2,1,0:T(8,128)(2,1)S(1)} %pad_maximum_fusion.u0_ref), channel_id=1, source_target_pairs={{0,384},{128,0},{256,128},{384,256},{1,385},{129,1},{257,129},{385... | collective-permute-start | bytes 1572872 | tf_op jit(solution)/shard_map/ppermute | solution.py:207
  113.3 2.5 %collective-permute-start.16 = (bf16[4,8,16,512]{3,2,1,0:T(8,128)(2,1)S(1)}, bf16[4,8,16,512]{3,2,1,0:T(8,128)(2,1)}, u32[]{:S(2)}, u32[]{:S(2)}) collective-permute-start(bf16[4,8,16,512]{3,2,1,0:T(8,128)(2,1)S(1)} %pad_maximum_fusion.1.l0_ref), channel_id=1, source_target_pairs={{0,128},{128,256},{256,384},{384,0},{1,129},{129,257},{257,385},{3... | collective-permute-start | bytes 1572872 | tf_op jit(solution)/shard_map/ppermute | solution.py:207
  115.7 12.6 %collective-permute-done.13.u3_ref = bf16[4,8,16,512]{3,2,1,0:T(8,128)(2,1)} collective-permute-done((bf16[4,8,16,512]{3,2,1,0:T(8,128)(2,1)S(1)}, bf16[4,8,16,512]{3,2,1,0:T(8,128)(2,1)}, u32[]{:S(2)}, u32[]{:S(2)}) %collective-permute-start.13) | collective-permute-done | bytes 524320 | tf_op jit(solution)/shard_map/ppermute | solution.py:207
  128.3 1.9 %collective-permute-start.14 = (bf16[4,8,16,512]{3,2,1,0:T(8,128)(2,1)}, bf16[4,8,16,512]{3,2,1,0:T(8,128)(2,1)}, u32[]{:S(2)}, u32[]{:S(2)}) collective-permute-start(bf16[4,8,16,512]{3,2,1,0:T(8,128)(2,1)} %collective-permute-done.13.u3_ref), channel_id=1, source_target_pairs={{0,128},{128,256},{256,384},{384,0},{1,129},{129,257},{257,385},{3... | collective-permute-start | bytes 1572872 | tf_op jit(solution)/shard_map/ppermute | solution.py:207
  130.2 0.0 collective-permute-done.12.l1_ref
  130.2 5.1 %collective-permute-start.15 = (bf16[4,8,16,512]{3,2,1,0:T(8,128)(2,1)S(1)}, bf16[4,8,16,512]{3,2,1,0:T(8,128)(2,1)}, u32[]{:S(2)}, u32[]{:S(2)}) collective-permute-start(bf16[4,8,16,512]{3,2,1,0:T(8,128)(2,1)S(1)} %collective-permute-done.12.l1_ref), channel_id=1, source_target_pairs={{0,384},{128,0},{256,128},{384,256},{1,385},{129,1},{257,129},{385... | collective-permute-start | bytes 1572872 | tf_op jit(solution)/shard_map/ppermute | solution.py:207
  135.4 0.7 pad_add_fusion.2.place_ref
  136.1 0.7 maximum_maximum_fusion.stream_ref
  136.8 0.0 all-to-all-done.1.in_ref
  136.8 1.0 copy-done
  137.8 2.6 %shard_map.97 = bf16[56,512]{1,0:T(8,128)(2,1)} custom-call(bf16[16,56,640]{2,1,0:T(8,128)(2,1)} %copy-done), custom_call_target="tpu_custom_call" | custom-call | flops 2000000000 | bytes 1200000 | tf_op jit(solution)/shard_map/pallas_call | solution.py:131
  140.4 15.7 %all-gather = bf16[224,512]{1,0:T(8,128)(2,1)} all-gather(bf16[56,512]{1,0:T(8,128)(2,1)} %shard_map.97), channel_id=2, replica_groups=mesh['y'=4,'z'=8,'x'=4,'h'=2,'c'=2] {'h','c'}, dimensions={0}, use_global_device_ids=true | all-gather | bytes 286720 | tf_op jit(solution)/shard_map/all_gather | solution.py:256
  156.1 0.0 collective-permute-done.11.u1_ref
  156.1 0.0 collective-permute-done.15.l2_ref
  156.1 0.0 copy-start.9
  156.2 0.0 copy-start.6
  156.2 5.8 %shard_map.98 = (bf16[48,1024]{1,0:T(8,128)(2,1)}, f32[2,56,320]{2,1,0:T(8,128)}, bf16[2,56,320]{2,1,0:T(8,128)(2,1)}) custom-call(s32[4]{0:T(128)} %pad_add_fusion.2.place_ref, bf16[4,56,512]{2,1,0:T(8,128)(2,1)} %bitcast.35, bf16[4,8,16,512]{3,2,1,0:T(8,128)(2,1)} %copy-done.2, bf16[4,8,16,512]{3,2,1,0:T(8,128)(2,1)} %copy-done.3, ...), custom_call_target="tpu_custom_call" | custom-call | flops 4000000000 | bytes 7000000 | tf_op jit(solution)/shard_map/pallas_call | solution.py:173
  162.0 2.2 %collective-permute-start.17 = (bf16[2,56,320]{2,1,0:T(8,128)(2,1)}, bf16[2,56,320]{2,1,0:T(8,128)(2,1)S(1)}, u32[]{:S(2)}, u32[]{:S(2)}) collective-permute-start(bf16[2,56,320]{2,1,0:T(8,128)(2,1)} %get-tuple-element.13), channel_id=1, source_target_pairs={{0,1},{1,0},{2,3},{3,2},{4,5},{5,4},{6,7},{7,6},{8,9},{9,8},{10,11... | collective-permute-start | bytes 215048 | tf_op jit(solution)/shard_map/ppermute | solution.py:230
  164.3 0.1 slice_bitcast_fusion.8
  164.3 1.0 collective-permute-done.17.arrived_ref
  165.4 0.6 copy-done.7
  166.0 1.6 shard_map.99
  167.6 5.5 %collective-permute-start.18 = (bf16[56,320]{1,0:T(8,128)(2,1)}, bf16[56,320]{1,0:T(8,128)(2,1)S(1)}, u32[]{:S(2)}, u32[]{:S(2)}) collective-permute-start(bf16[56,320]{1,0:T(8,128)(2,1)} %get-tuple-element.15), channel_id=1, source_target_pairs={{0,2},{2,0},{1,3},{3,1},{4,6},{6,4},{5,7},{7,5},{8,10},{10,8},{9,1... | collective-permute-start | bytes 107528 | tf_op jit(solution)/shard_map/ppermute | solution.py:230
  173.1 0.1 pad_add_fusion.1
  173.2 10.3 %collective-permute-done.18 = bf16[56,320]{1,0:T(8,128)(2,1)S(1)} collective-permute-done((bf16[56,320]{1,0:T(8,128)(2,1)}, bf16[56,320]{1,0:T(8,128)(2,1)S(1)}, u32[]{:S(2)}, u32[]{:S(2)}) %collective-permute-start.18) | collective-permute-done | bytes 35872 | tf_op jit(solution)/shard_map/ppermute | solution.py:230
  183.5 1.7 fusion
  (33 shorter events, 0.2 us)
Async XLA Ops:
  2.4 17.7 %collective-permute-start = (bf16[1,1536]{1,0:T(2,128)(2,1)}, bf16[1,1536]{1,0:T(2,128)(2,1)S(1)}, u32[]{:S(2)}, u32[]{:S(2)}) collective-permute-start(bf16[1,1536]{1,0:T(2,128)(2,1)} %get-tuple-element.9), channel_id=1, source_target_pairs={{0,4},{4,8},{8,12},{12,16},{16,20},{20,24},{24,28},{28,32},{32,36}... | collective-permute-start | bytes 9224 | tf_op jit(solution)/shard_map/ppermute | solution.py:241
  5.5 55.9 %collective-permute-start.1 = (bf16[1,48,1024]{2,1,0:T(8,128)(2,1)}, bf16[1,48,1024]{2,1,0:T(8,128)(2,1)S(1)}, u32[]{:S(2)}, u32[]{:S(2)}) collective-permute-start(bf16[1,48,1024]{2,1,0:T(8,128)(2,1)} %get-tuple-element.10), channel_id=1, source_target_pairs={{0,64},{16,80},{32,96},{48,112},{64,0},{80,16},{96,32},{112,48},{1... | collective-permute-start | bytes 294920 | tf_op jit(solution)/shard_map/ppermute | solution.py:213
  14.6 2.9 %collective-permute-start.4 = (bf16[32,512]{1,0:T(8,128)(2,1)}, bf16[32,512]{1,0:T(8,128)(2,1)S(1)}, u32[]{:S(2)}, u32[]{:S(2)}) collective-permute-start(bf16[32,512]{1,0:T(8,128)(2,1)} %bitcast.38), channel_id=1, source_target_pairs={{0,0},{1,128},{2,256},{3,384},{128,1},{129,129},{130,257},{131,385... | collective-permute-start | bytes 98312 | tf_op jit(solution)/shard_map/ppermute | solution.py:237
  17.6 9.7 %collective-permute-start.5 = (bf16[1,32,512]{2,1,0:T(8,128)(2,1)S(1)}, bf16[1,32,512]{2,1,0:T(8,128)(2,1)S(1)}, u32[]{:S(2)}, u32[]{:S(2)}) collective-permute-start(bf16[1,32,512]{2,1,0:T(8,128)(2,1)S(1)} %bitcast.31), channel_id=1, source_target_pairs={{0,64},{16,80},{32,96},{48,112},{64,0},{80,16},{96,32},{112,48},{1... | collective-permute-start | bytes 98312 | tf_op jit(solution)/shard_map/ppermute | solution.py:213
  27.3 29.4 %collective-permute-start.6 = (bf16[2,32,512]{2,1,0:T(8,128)(2,1)S(1)}, bf16[2,32,512]{2,1,0:T(8,128)(2,1)S(1)}, u32[]{:S(2)}, u32[]{:S(2)}) collective-permute-start(bf16[2,32,512]{2,1,0:T(8,128)(2,1)S(1)} %pad_maximum_fusion.5), channel_id=1, source_target_pairs={{0,32},{16,48},{32,0},{48,16},{64,96},{80,112},{96,64},{112,80},{1... | collective-permute-start | bytes 196616 | tf_op jit(solution)/shard_map/ppermute | solution.py:213
  34.4 27.1 %copy-start.5 = (bf16[1,48,1024]{2,1,0:T(8,128)(2,1)S(1)}, bf16[1,48,1024]{2,1,0:T(8,128)(2,1)}, u32[]{:S(2)}) copy-start(bf16[1,48,1024]{2,1,0:T(8,128)(2,1)} %get-tuple-element.10) | copy-start | bytes 294916
  34.4 52.2 %all-to-all-start = ((bf16[16,56,512]{2,1,0:T(8,128)(2,1)}), bf16[16,56,512]{2,1,0:T(8,128)(2,1)S(1)}, u32[]{:S(2)}, u32[]{:S(2)}) async-start(bf16[16,56,512]{2,1,0:T(8,128)(2,1)} %broadcast_in_dim.11), calls=%async_computation | async-start | bytes 1835008 | tf_op jit(solution)/shard_map/all_to_all | solution.py:141
  56.7 9.0 %collective-permute-start.7 = (bf16[4,32,512]{2,1,0:T(8,128)(2,1)S(1)}, bf16[4,32,512]{2,1,0:T(8,128)(2,1)S(1)}, u32[]{:S(2)}, u32[]{:S(2)}) collective-permute-start(bf16[4,32,512]{2,1,0:T(8,128)(2,1)S(1)} %pad_maximum_fusion.4), channel_id=1, source_target_pairs={{0,16},{16,0},{32,48},{48,32},{64,80},{80,64},{96,112},{112,96},{1... | collective-permute-start | bytes 393224 | tf_op jit(solution)/shard_map/ppermute | solution.py:213
  61.5 13.3 %collective-permute-start.2 = (bf16[2,48,1024]{2,1,0:T(8,128)(2,1)S(1)}, bf16[2,48,1024]{2,1,0:T(8,128)(2,1)S(1)}, u32[]{:S(2)}, u32[]{:S(2)}) collective-permute-start(bf16[2,48,1024]{2,1,0:T(8,128)(2,1)S(1)} %pad_maximum_fusion.3), channel_id=1, source_target_pairs={{0,32},{16,48},{32,0},{48,16},{64,96},{80,112},{96,64},{112,80},{1... | collective-permute-start | bytes 589832 | tf_op jit(solution)/shard_map/ppermute | solution.py:213
  65.8 12.9 %collective-permute-start.10 = (bf16[8,32,512]{2,1,0:T(8,128)(2,1)S(1)}, bf16[8,32,512]{2,1,0:T(8,128)(2,1)S(1)}, u32[]{:S(2)}, u32[]{:S(2)}) collective-permute-start(bf16[8,32,512]{2,1,0:T(8,128)(2,1)S(1)} %pad_maximum_fusion.2), channel_id=1, source_target_pairs={{0,12},{4,0},{8,4},{12,8},{1,13},{5,1},{9,5},{13,9},{2,14},{6,2},{... | collective-permute-start | bytes 786440 | tf_op jit(solution)/shard_map/ppermute | solution.py:207
  68.3 11.4 %collective-permute-start.9 = (bf16[8,32,512]{2,1,0:T(8,128)(2,1)S(1)}, bf16[8,32,512]{2,1,0:T(8,128)(2,1)S(1)}, u32[]{:S(2)}, u32[]{:S(2)}) collective-permute-start(bf16[8,32,512]{2,1,0:T(8,128)(2,1)S(1)} %pad_maximum_fusion.2), channel_id=1, source_target_pairs={{0,8},{4,12},{8,0},{12,4},{1,9},{5,13},{9,1},{13,5},{2,10},{6,14},... | collective-permute-start | bytes 786440 | tf_op jit(solution)/shard_map/ppermute | solution.py:207
  72.9 9.5 %collective-permute-start.8 = (bf16[8,32,512]{2,1,0:T(8,128)(2,1)S(1)}, bf16[8,32,512]{2,1,0:T(8,128)(2,1)S(1)}, u32[]{:S(2)}, u32[]{:S(2)}) collective-permute-start(bf16[8,32,512]{2,1,0:T(8,128)(2,1)S(1)} %pad_maximum_fusion.2), channel_id=1, source_target_pairs={{0,4},{4,8},{8,12},{12,0},{1,5},{5,9},{9,13},{13,1},{2,6},{6,10},{... | collective-permute-start | bytes 786440 | tf_op jit(solution)/shard_map/ppermute | solution.py:207
  74.9 11.7 %copy-start.8 = (bf16[4,48,1024]{2,1,0:T(8,128)(2,1)}, bf16[4,48,1024]{2,1,0:T(8,128)(2,1)S(1)}, u32[]{:S(2)}) copy-start(bf16[4,48,1024]{2,1,0:T(8,128)(2,1)S(1)} %constant_dynamic-update-slice_fusion.near_ref) | copy-start | bytes 1179652
  74.9 11.7 %collective-permute-start.3 = (bf16[4,48,1024]{2,1,0:T(8,128)(2,1)S(1)}, bf16[4,48,1024]{2,1,0:T(8,128)(2,1)}, u32[]{:S(2)}, u32[]{:S(2)}) collective-permute-start(bf16[4,48,1024]{2,1,0:T(8,128)(2,1)S(1)} %constant_dynamic-update-slice_fusion.near_ref), channel_id=1, source_target_pairs={{0,16},{16,0},{32,48},{48,32},{64,80},{80,64},{96,112},{112,96},{1... | collective-permute-start | bytes 1179656 | tf_op jit(solution)/shard_map/ppermute | solution.py:213
  86.6 0.9 copy-start.1
  95.4 41.4 %all-to-all-start.1 = ((bf16[16,56,640]{2,1,0:T(8,128)(2,1)}), bf16[16,56,640]{2,1,0:T(8,128)(2,1)S(1)}, u32[]{:S(2)}, u32[]{:S(2)}) async-start(bf16[16,56,640]{2,1,0:T(8,128)(2,1)} %shard_map.96), calls=%async_computation.1 | async-start | bytes 2293760 | tf_op jit(solution)/shard_map/all_to_all | solution.py:141
  102.6 33.4 %copy-start.4 = (bf16[48,1024]{1,0:T(8,128)(2,1)S(1)}, bf16[48,1024]{1,0:T(8,128)(2,1)}, u32[]{:S(2)}) copy-start(bf16[48,1024]{1,0:T(8,128)(2,1)} %stream_ref.1) | copy-start | bytes 294916
  102.7 37.7 %copy-start.2 = (bf16[4,8,16,512]{3,2,1,0:T(8,128)(2,1)}, bf16[4,8,16,512]{3,2,1,0:T(8,128)(2,1)S(1)}, u32[]{:S(2)}) copy-start(bf16[4,8,16,512]{3,2,1,0:T(8,128)(2,1)S(1)} %pad_maximum_fusion.u0_ref) | copy-start | bytes 1572868
  102.7 25.6 %collective-permute-start.13 = (bf16[4,8,16,512]{3,2,1,0:T(8,128)(2,1)S(1)}, bf16[4,8,16,512]{3,2,1,0:T(8,128)(2,1)}, u32[]{:S(2)}, u32[]{:S(2)}) collective-permute-start(bf16[4,8,16,512]{3,2,1,0:T(8,128)(2,1)S(1)} %pad_maximum_fusion.u0_ref), channel_id=1, source_target_pairs={{0,128},{128,256},{256,384},{384,0},{1,129},{129,257},{257,385},{3... | collective-permute-start | bytes 1572872 | tf_op jit(solution)/shard_map/ppermute | solution.py:207
  106.2 34.3 %copy-start.3 = (bf16[4,8,16,512]{3,2,1,0:T(8,128)(2,1)}, bf16[4,8,16,512]{3,2,1,0:T(8,128)(2,1)S(1)}, u32[]{:S(2)}) copy-start(bf16[4,8,16,512]{3,2,1,0:T(8,128)(2,1)S(1)} %pad_maximum_fusion.1.l0_ref) | copy-start | bytes 1572868
  106.2 24.0 %collective-permute-start.12 = (bf16[4,8,16,512]{3,2,1,0:T(8,128)(2,1)S(1)}, bf16[4,8,16,512]{3,2,1,0:T(8,128)(2,1)S(1)}, u32[]{:S(2)}, u32[]{:S(2)}) collective-permute-start(bf16[4,8,16,512]{3,2,1,0:T(8,128)(2,1)S(1)} %pad_maximum_fusion.1.l0_ref), channel_id=1, source_target_pairs={{0,384},{128,0},{256,128},{384,256},{1,385},{129,1},{257,129},{385... | collective-permute-start | bytes 1572872 | tf_op jit(solution)/shard_map/ppermute | solution.py:207
  109.9 46.3 %collective-permute-start.11 = (bf16[4,8,16,512]{3,2,1,0:T(8,128)(2,1)S(1)}, bf16[4,8,16,512]{3,2,1,0:T(8,128)(2,1)}, u32[]{:S(2)}, u32[]{:S(2)}) collective-permute-start(bf16[4,8,16,512]{3,2,1,0:T(8,128)(2,1)S(1)} %pad_maximum_fusion.u0_ref), channel_id=1, source_target_pairs={{0,384},{128,0},{256,128},{384,256},{1,385},{129,1},{257,129},{385... | collective-permute-start | bytes 1572872 | tf_op jit(solution)/shard_map/ppermute | solution.py:207
  113.3 42.9 %collective-permute-start.16 = (bf16[4,8,16,512]{3,2,1,0:T(8,128)(2,1)S(1)}, bf16[4,8,16,512]{3,2,1,0:T(8,128)(2,1)}, u32[]{:S(2)}, u32[]{:S(2)}) collective-permute-start(bf16[4,8,16,512]{3,2,1,0:T(8,128)(2,1)S(1)} %pad_maximum_fusion.1.l0_ref), channel_id=1, source_target_pairs={{0,128},{128,256},{256,384},{384,0},{1,129},{129,257},{257,385},{3... | collective-permute-start | bytes 1572872 | tf_op jit(solution)/shard_map/ppermute | solution.py:207
  128.3 27.8 %collective-permute-start.14 = (bf16[4,8,16,512]{3,2,1,0:T(8,128)(2,1)}, bf16[4,8,16,512]{3,2,1,0:T(8,128)(2,1)}, u32[]{:S(2)}, u32[]{:S(2)}) collective-permute-start(bf16[4,8,16,512]{3,2,1,0:T(8,128)(2,1)} %collective-permute-done.13.u3_ref), channel_id=1, source_target_pairs={{0,128},{128,256},{256,384},{384,0},{1,129},{129,257},{257,385},{3... | collective-permute-start | bytes 1572872 | tf_op jit(solution)/shard_map/ppermute | solution.py:207
  130.2 10.2 %copy-start.10 = (bf16[4,8,16,512]{3,2,1,0:T(8,128)(2,1)}, bf16[4,8,16,512]{3,2,1,0:T(8,128)(2,1)S(1)}, u32[]{:S(2)}) copy-start(bf16[4,8,16,512]{3,2,1,0:T(8,128)(2,1)S(1)} %collective-permute-done.12.l1_ref) | copy-start | bytes 1572868
  130.2 25.9 %collective-permute-start.15 = (bf16[4,8,16,512]{3,2,1,0:T(8,128)(2,1)S(1)}, bf16[4,8,16,512]{3,2,1,0:T(8,128)(2,1)}, u32[]{:S(2)}, u32[]{:S(2)}) collective-permute-start(bf16[4,8,16,512]{3,2,1,0:T(8,128)(2,1)S(1)} %collective-permute-done.12.l1_ref), channel_id=1, source_target_pairs={{0,384},{128,0},{256,128},{384,256},{1,385},{129,1},{257,129},{385... | collective-permute-start | bytes 1572872 | tf_op jit(solution)/shard_map/ppermute | solution.py:207
  136.8 1.0 copy-start
  156.1 8.1 %copy-start.9 = (s32[1,48]{1,0:T(1,128)S(1)}, s32[1,48]{1,0:T(1,128)}, u32[]{:S(2)}) copy-start(s32[1,48]{1,0:T(1,128)} %starts_ref.1) | copy-start | bytes 580
  156.2 27.3 %copy-start.6 = (bf16[192,320]{1,0:T(8,128)(2,1)S(1)}, bf16[192,320]{1,0:T(8,128)(2,1)}, u32[]{:S(2)}) copy-start(bf16[192,320]{1,0:T(8,128)(2,1)} %param.14) | copy-start | bytes 368644
  162.0 3.4 %collective-permute-start.17 = (bf16[2,56,320]{2,1,0:T(8,128)(2,1)}, bf16[2,56,320]{2,1,0:T(8,128)(2,1)S(1)}, u32[]{:S(2)}, u32[]{:S(2)}) collective-permute-start(bf16[2,56,320]{2,1,0:T(8,128)(2,1)} %get-tuple-element.13), channel_id=1, source_target_pairs={{0,1},{1,0},{2,3},{3,2},{4,5},{5,4},{6,7},{7,6},{8,9},{9,8},{10,11... | collective-permute-start | bytes 215048 | tf_op jit(solution)/shard_map/ppermute | solution.py:230
  165.4 0.6 copy-start.7
  167.6 15.8 %collective-permute-start.18 = (bf16[56,320]{1,0:T(8,128)(2,1)}, bf16[56,320]{1,0:T(8,128)(2,1)S(1)}, u32[]{:S(2)}, u32[]{:S(2)}) collective-permute-start(bf16[56,320]{1,0:T(8,128)(2,1)} %get-tuple-element.15), channel_id=1, source_target_pairs={{0,2},{2,0},{1,3},{3,1},{4,6},{6,4},{5,7},{7,5},{8,10},{10,8},{9,1... | collective-permute-start | bytes 107528 | tf_op jit(solution)/shard_map/ppermute | solution.py:230
